TPU v7x, 32 devices: a whole 2x2x4 slice. The times are simulated.
32 devices in a mesh: dp: 4 (over z), seq: 4 (over y, core), tp: 2 (over x).
Axes of the slice: x: 2, y: 2, z: 4, core: 2. Of those that a mesh axis runs over, the one named last changes fastest.
Arguments:
- queries: bfloat16 [8192, 1024], P(('dp', 'seq'), 'tp'), parts along dimension 0, may hold values from -181 to 181
- rotated_key_states: bfloat16 [8192, 256], P(('dp', 'seq'), 'tp'), parts along dimension 0, may hold values from -6.1 to 6.1
- value_state_vectors: bfloat16 [8192, 256], P(('dp', 'seq'), 'tp'), parts along dimension 0, may hold values from -6 to 6
- out_weight: bfloat16 [1024, 8192], P('tp'), may hold values from -0.3125 to 0.3125
- residual: bfloat16 [8192, 8192], P(('dp', 'seq', 'tp')), parts along dimension 0, may hold values from -0.75 to 0.75
- norm_gain: bfloat16 [8192], replicated, may hold values from 0.099609375 to 2
Outputs:
- new_residual: bfloat16 [8192, 8192], P(('dp', 'seq', 'tp')), parts along dimension 0
- next_input: bfloat16 [8192, 8192], P(('dp', 'seq', 'tp')), parts along dimension 0
There are 4 independent parts, one for each index of `dp`. A program takes and returns all parts, laid end to end along the dimension named above; an argument that names none is the same for every part. Nothing has to cross between parts.
All inputs are finite; a program needn't handle non-finite values.
Results may differ from a plain program's by a relative error of at most 0.025.
Values may be sent and summed in bfloat16 or wider, within the bound.
A program may use at most 192 MiB of HBM per device.

v0:
```python
import functools

import jax
import jax.numpy as jnp
from jax import lax
from jax.experimental import pallas as pl
from jax.experimental.pallas import tpu as pltpu
from jax.sharding import PartitionSpec as P

HEAD_SIZE = 128
BLOCK = 16
softness = 0.9
scale_floor = 256.0
neg_large = -1e30
ROUND_BIG = 12582912.0
Q_COEFFS = (0.8999997814, -0.5804296733, 0.1500389216, -0.0212977078, 0.0016888914)


def soft_grid(u):
    turns = (u * 0.5 + ROUND_BIG) - ROUND_BIG
    t = u - (turns + turns)
    z = t * t
    q = jnp.float32(Q_COEFFS[-1])
    for c in Q_COEFFS[-2::-1]:
        q = q * z + jnp.float32(c)
    return u - (t - t * z) * q


def spacing_of(block_max, peak):
    tensor_scale = peak / (6.0 * 448.0)
    inv = 1.0 / (6.0 * tensor_scale)
    scale = jnp.maximum(block_max * inv, scale_floor).astype(jnp.bfloat16)
    return scale, tensor_scale


def quant_rows(x, peak):
    rows, cols = x.shape
    xb = x.reshape(rows // BLOCK, BLOCK, cols)
    block_max = jnp.max(jnp.abs(xb), axis=1, keepdims=True)
    scale, tensor_scale = spacing_of(block_max, peak)
    spacing = scale.astype(jnp.float32) * tensor_scale
    payload = soft_grid(xb * (1.0 / spacing)).astype(jnp.bfloat16).astype(jnp.float32)
    return (payload * spacing).reshape(rows, cols)


def quant_kernel(peak_ref, w_ref, out_ref, *, unroll):
    peak = peak_ref[0, 0]
    rows = w_ref.shape[0]

    def step(i, carry):
        sl = pl.ds(pl.multiple_of(i * BLOCK, BLOCK), BLOCK)
        out_ref[sl, :] = quant_rows(w_ref[sl, :].astype(jnp.float32), peak).astype(jnp.bfloat16)
        return carry

    lax.fori_loop(0, rows // BLOCK, step, 0, unroll=unroll)


def quant_weight(w, peak, width, first, cols):
    rows = w.shape[0]
    skip = first // width
    return pl.pallas_call(
        functools.partial(quant_kernel, unroll=4),
        grid=(cols // width,),
        in_specs=[
            pl.BlockSpec(memory_space=pltpu.SMEM),
            pl.BlockSpec((rows, width), lambda i: (0, i + skip)),
        ],
        out_specs=pl.BlockSpec((rows, width), lambda i: (0, i)),
        out_shape=jax.ShapeDtypeStruct((rows, cols), jnp.bfloat16),
        cost_estimate=pl.CostEstimate(
            flops=40 * rows * cols, bytes_accessed=4 * rows * cols, transcendentals=0
        ),
        name="quant_weight",
    )(peak, w)


def project_kernel(*refs, n_tp, n_feat, n_alias, features):
    peak_ref, act_refs = refs[0], refs[1 : 1 + n_tp]
    own_ref, peer_ref, res_ref, gain_ref, sq_in, top_in = refs[1 + n_tp : 7 + n_tp]
    refs = refs[7 + n_tp + n_alias :]
    new_ref, hid_ref, square_sum, row_top, rstd_ref, top_ref, act_q = refs
    step_id = pl.program_id(0)

    @pl.when(step_id == 0)
    def _():
        peak = peak_ref[0, 0]
        square_sum[...] = sq_in[...]
        row_top[...] = top_in[...]
        for k in range(n_tp):
            for lo in range(0, n_feat, 128):
                x = act_refs[k][lo : lo + 128, :].astype(jnp.float32)
                act_q[k, :, lo : lo + 128] = quant_rows(x, peak).T.astype(jnp.bfloat16)

    hidden = res_ref[...].astype(jnp.float32)
    for k in range(n_tp):
        w = own_ref[...] if k == 0 else peer_ref[0, k - 1]
        part = jnp.dot(act_q[k], w, preferred_element_type=jnp.float32)
        hidden = hidden + part.astype(jnp.bfloat16).astype(jnp.float32)
    new_ref[...] = hidden.astype(jnp.bfloat16)
    hid_ref[...] = hidden
    sq = square_sum[...]
    top = row_top[...]
    scaled = jnp.abs(hidden * gain_ref[...])
    for lo in range(0, hidden.shape[1], 128):
        part = hidden[:, lo : lo + 128]
        sq = sq + part * part
        top = jnp.maximum(top, scaled[:, lo : lo + 128])
    square_sum[...] = sq
    row_top[...] = top

    @pl.when(step_id == pl.num_programs(0) - 1)
    def _():
        mean_square = jnp.sum(square_sum[...], axis=1, keepdims=True) / features
        rstd = lax.rsqrt(mean_square + 1e-05)
        rstd_ref[...] = jnp.broadcast_to(rstd, rstd_ref.shape)
        top_all = jnp.max(jnp.max(row_top[...], axis=1, keepdims=True) * rstd)
        top_ref[...] = jnp.full(top_ref.shape, top_all, jnp.float32)


def project(peak, acts, w_own, w_peer, residual, gain, stats, width, skip, wide, made):
    n_tp = len(acts)
    n_feat, tokens = acts[0].shape
    d = residual.shape[1]
    steps = w_own.shape[1] // width
    column = pl.BlockSpec((tokens, width), lambda i: (0, i + skip))
    whole = pl.BlockSpec((tokens, 128), lambda i: (0, 0))
    if wide:
        peer_spec = pl.BlockSpec((1, n_tp - 1, n_feat, width), lambda i: (0, 0, 0, i))
    else:
        peer_spec = pl.BlockSpec((1, n_tp - 1, n_feat, width), lambda i: (i, 0, 0, 0))
    stat = jax.ShapeDtypeStruct((tokens, 128), jnp.float32)
    return pl.pallas_call(
        functools.partial(project_kernel, n_tp=n_tp, n_feat=n_feat, n_alias=len(made), features=d),
        grid=(steps,),
        in_specs=[pl.BlockSpec(memory_space=pltpu.SMEM)]
        + [pl.BlockSpec((n_feat, tokens), lambda i: (0, 0))] * n_tp
        + [
            pl.BlockSpec((n_feat, width), lambda i: (0, i)),
            peer_spec,
            column,
            pl.BlockSpec((1, width), lambda i: (0, i + skip)),
            whole,
            whole,
        ]
        + [pl.BlockSpec(memory_space=pl.ANY)] * len(made),
        out_specs=[column, column, whole, whole, whole, pl.BlockSpec((8, 128), lambda i: (0, 0))],
        out_shape=[
            jax.ShapeDtypeStruct((tokens, d), jnp.bfloat16),
            jax.ShapeDtypeStruct((tokens, d), jnp.float32),
            stat,
            stat,
            stat,
            jax.ShapeDtypeStruct((8, 128), jnp.float32),
        ],
        input_output_aliases={7 + n_tp + i: i for i in range(len(made))},
        scratch_shapes=[pltpu.VMEM((n_tp, tokens, n_feat), jnp.bfloat16)],
        cost_estimate=pl.CostEstimate(
            flops=2 * n_tp * n_feat * tokens * steps * width,
            bytes_accessed=2 * n_tp * n_feat * steps * width,
            transcendentals=0,
        ),
        name="project",
    )(peak, *acts, w_own, w_peer, residual, gain, *stats, *made)


def final_kernel(peak_ref, hid_ref, rstd_ref, gain_ref, out_ref, narrow, wide):
    peak = peak_ref[0, 0]
    rows, cols = hid_ref.shape
    src = lax.broadcasted_iota(jnp.int32, (128, 128), 0)
    dst = lax.broadcasted_iota(jnp.int32, (128, 128), 1)
    spread = jnp.where(src == (dst // BLOCK) * BLOCK + BLOCK - 1, 1.0, 0.0).astype(jnp.bfloat16)
    rstd = rstd_ref[...]
    tensor_scale = peak / (6.0 * 448.0)
    pieces = cols // 128
    for i in range(pieces):
        x = hid_ref[:, i * 128 : i * 128 + 128] * rstd * gain_ref[:, i * 128 : i * 128 + 128]
        m = jnp.abs(x)
        for s in (1, 2, 4, 8):
            m = jnp.maximum(m, pltpu.roll(m, s, 1))
        narrow[i * rows : (i + 1) * rows, :] = spacing_of(m, peak)[0]
    wide[...] = jnp.dot(narrow[...], spread, preferred_element_type=jnp.float32)
    for i in range(pieces):
        x = hid_ref[:, i * 128 : i * 128 + 128] * rstd * gain_ref[:, i * 128 : i * 128 + 128]
        spacing = wide[i * rows : (i + 1) * rows, :] * tensor_scale
        payload = soft_grid(x * pl.reciprocal(spacing)).astype(jnp.bfloat16).astype(jnp.float32)
        out_ref[:, i * 128 : i * 128 + 128] = (payload * spacing).astype(jnp.bfloat16)


def final_quant(peak, hidden, rstd, gain):
    tokens, d = hidden.shape
    width = 2048
    rows = min(64, tokens)
    column = pl.BlockSpec((rows, width), lambda i, j: (i, j))
    return pl.pallas_call(
        final_kernel,
        grid=(tokens // rows, d // width),
        in_specs=[
            pl.BlockSpec(memory_space=pltpu.SMEM),
            column,
            pl.BlockSpec((rows, 128), lambda i, j: (i, 0)),
            pl.BlockSpec((1, width), lambda i, j: (0, j)),
        ],
        out_specs=column,
        out_shape=jax.ShapeDtypeStruct((tokens, d), jnp.bfloat16),
        scratch_shapes=[
            pltpu.VMEM((rows * width // 128, 128), jnp.bfloat16),
            pltpu.VMEM((rows * width // 128, 128), jnp.float32),
        ],
        name="final_quant",
    )(peak, hidden, rstd, gain)


def attend(queries, keys, values, first_query):
    token_count = queries.shape[0]
    kv_heads = keys.shape[1] // HEAD_SIZE
    grouped = queries.shape[1] // HEAD_SIZE // kv_heads
    q = queries.reshape(token_count, kv_heads, grouped, HEAD_SIZE)
    k = keys.reshape(-1, kv_heads, HEAD_SIZE)
    v = values.reshape(-1, kv_heads, HEAD_SIZE)
    scores = jnp.einsum("tkgd,skd->kgts", q, k, preferred_element_type=jnp.float32)
    scores = scores * HEAD_SIZE ** (-0.5)
    query_pos = first_query + lax.broadcasted_iota(jnp.int32, (token_count, 1), 0)
    key_pos = lax.broadcasted_iota(jnp.int32, (1, k.shape[0]), 1)
    allowed = query_pos >= key_pos
    masked = jnp.where(allowed, scores, neg_large)
    top = jnp.max(masked, axis=3, keepdims=True)
    weights = jnp.where(allowed, jnp.exp(masked - top), 0.0)
    total = jnp.sum(weights, axis=3)
    summed = jnp.einsum(
        "kgts,skd->kgtd", weights.astype(jnp.bfloat16), v, preferred_element_type=jnp.float32
    )
    attended = (summed / total[..., None]).astype(jnp.bfloat16)
    return attended.transpose(0, 1, 3, 2).reshape(-1, token_count)


def local(queries, keys, values, out_weight, residual, norm_gain):
    token_count = queries.shape[0]
    n_tp = lax.axis_size("tp")
    tp_rank = lax.axis_index("tp")
    slabs = lax.axis_size("dp") * lax.axis_size("seq")
    d = out_weight.shape[1]
    width = d // slabs
    kv = lax.all_gather(jnp.stack((keys, values)), "seq", axis=1, tiled=True)

    weight_top = jnp.max(jnp.abs(out_weight)).astype(jnp.float32)
    weight_peak = lax.pmax(weight_top, "tp").reshape(1, 1)
    slab_id = lax.axis_index("dp") * lax.axis_size("seq") + lax.axis_index("seq")
    direct = 128
    gather_w = width - direct
    gathered = slabs * gather_w
    slab = lax.dynamic_slice_in_dim(out_weight, slab_id * gather_w, gather_w, axis=1)
    slab_q = quant_weight(slab, weight_peak, gather_w, 0, gather_w)
    shifts = [[(i, (i + k) % n_tp) for i in range(n_tp)] for k in range(1, n_tp)]
    from_peers = jnp.stack([lax.ppermute(slab_q, "tp", ring) for ring in shifts])
    w_peer = lax.all_gather(from_peers, ("dp", "seq"), axis=0)
    near_own = quant_weight(out_weight, weight_peak, 512, gathered, d - gathered)
    near_peer = jnp.stack([lax.ppermute(near_own, "tp", ring) for ring in shifts])[None]
    w_own = quant_weight(out_weight, weight_peak, gather_w, 0, gathered)

    act_t = attend(queries, kv[0], kv[1], lax.axis_index("seq") * token_count)
    act_top = jnp.max(jnp.abs(act_t)).astype(jnp.float32)
    share = token_count // n_tp
    pieces = []
    for k in range(n_tp):
        whose = lax.rem(tp_rank + k, n_tp)
        piece = lax.dynamic_slice_in_dim(act_t, whose * share, share, axis=1)
        pieces.append(piece if k == 0 else lax.ppermute(piece, "tp", shifts[k - 1]))
    act_peak = lax.pmax(act_top, ("seq", "tp")).reshape(1, 1)

    gain = norm_gain.astype(jnp.float32).reshape(1, d)
    stats = (jnp.zeros((share, 128), jnp.float32),) * 2
    near = project(
        act_peak, pieces, near_own, near_peer, residual, gain, stats, 512, gathered // 512, True, ()
    )
    new_residual, hidden, _, _, rstd, top = project(
        act_peak, pieces, w_own, w_peer, residual, gain, near[2:4], gather_w, 0, False, near[:2]
    )
    norm_peak = lax.pmax(top[0, 0], ("seq", "tp")).reshape(1, 1)
    next_input = final_quant(norm_peak, hidden, rstd, gain)
    return (new_residual, next_input)


def solution(mesh):
    in_specs = (
        P(("dp", "seq"), "tp"),
        P(("dp", "seq"), "tp"),
        P(("dp", "seq"), "tp"),
        P("tp", None),
        P(("dp", "seq", "tp"), None),
        P(),
    )
    out_specs = (P(("dp", "seq", "tp"), None), P(("dp", "seq", "tp"), None))
    return jax.shard_map(local, mesh=mesh, in_specs=in_specs, out_specs=out_specs, check_vma=False)
```

profile of v0, /device:TPU:0, one launch (start us, length us, event | category | flops | bytes accessed | tf_op | source)
XLA Modules:
  0.0 175.9 jit_solution(2849412599000884221)
XLA Ops:
  7.2 0.0 copy-start
  7.2 0.0 all-gather.4.cloned.1.call-start
  7.2 1.7 pad_maximum_fusion
  9.0 0.0 all-gather.4.cloned.1.call-update
  9.0 0.0 all-gather.6.cloned.1.call-start
  9.1 5.1 %abs_reduce_fusion = bf16[]{:T(256)} fusion(bf16[512,8192]{1,0:T(8,128)(2,1)} %w_ref.3), kind=kLoop, calls=%fused_computation.6 | loop fusion | flops 8388607 | bytes 8388610 | tf_op jit(solution)/shard_map/reduce_max | solution.py:245
  14.2 6.5 %pmax.22.peak_ref = f32[1,1]{1,0:T(1,128)} all-reduce(bf16[1,1]{1,0:T(2,128)(2,1)} %bitcast.22), channel_id=1, replica_groups=mesh['dp'=4,'seq'=4,'tp'=2] {'tp'}, use_global_device_ids=true, to_apply=%region_5.6 | all-reduce | flops 1 | bytes 6 | tf_op jit(solution)/shard_map/pmax | solution.py:246
  20.7 1.8 %constant_dynamic-slice_fusion.w_ref = bf16[512,384]{1,0:T(8,128)(2,1)} fusion(bf16[512,8192]{1,0:T(8,128)(2,1)} %w_ref.3, s32[]{:T(128)S(6)} %select_n.20), kind=kLoop, calls=%fused_computation.20 | loop fusion | bytes 786436 | tf_op jit(solution)/shard_map/dynamic_slice | solution.py:251
  22.5 3.4 %quant_weight.4 = bf16[512,384]{1,0:T(8,128)(2,1)} custom-call(f32[1,1]{1,0:T(1,128)} %pmax.22.peak_ref, bf16[512,384]{1,0:T(8,128)(2,1)} %constant_dynamic-slice_fusion.w_ref), custom_call_target="tpu_custom_call" | custom-call | flops 7864320 | bytes 786432 | tf_op jit(solution)/shard_map/quant_weight/pallas_call | solution.py:61
  25.9 2.0 %collective-permute-start.1 = (bf16[512,384]{1,0:T(8,128)(2,1)}, bf16[512,384]{1,0:T(8,128)(2,1)S(1)}, u32[]{:S(2)}, u32[]{:S(2)}) collective-permute-start(bf16[512,384]{1,0:T(8,128)(2,1)} %quant_weight.4), channel_id=1, source_target_pairs={{0,1},{1,0},{2,3},{3,2},{4,5},{5,4},{6,7},{7,6},{8,9},{9,8},{10,11... | collective-permute-start | bytes 1179656 | tf_op jit(solution)/shard_map/ppermute | solution.py:254
  28.0 8.2 %collective-permute-done.1 = bf16[512,384]{1,0:T(8,128)(2,1)S(1)} collective-permute-done((bf16[512,384]{1,0:T(8,128)(2,1)}, bf16[512,384]{1,0:T(8,128)(2,1)S(1)}, u32[]{:S(2)}, u32[]{:S(2)}) %collective-permute-start.1) | collective-permute-done | bytes 393248 | tf_op jit(solution)/shard_map/ppermute | solution.py:254
  36.2 0.0 copy-start.3
  36.2 0.8 copy-done.3
  36.9 0.0 all-gather.6.cloned.1.call-update
  37.0 7.6 %quant_weight.5.refs_3_ = bf16[512,2048]{1,0:T(8,128)(2,1)} custom-call(f32[1,1]{1,0:T(1,128)} %pmax.22.peak_ref, bf16[512,8192]{1,0:T(8,128)(2,1)} %w_ref.3), custom_call_target="tpu_custom_call" | custom-call | flops 41943040 | bytes 4194304 | tf_op jit(solution)/shard_map/quant_weight/pallas_call | solution.py:61
  44.5 1.7 collective-permute-start.2
  46.3 0.8 iota_compare_fusion
  47.1 0.0 all-gather.4.cloned.1.call-done
  47.1 0.0 copy-done
  47.1 0.0 copy-start.5
  47.1 4.3 %fusion = (f32[4,512]{1,0:T(4,128)S(1)}, f32[2048,512,4]{1,0,2:T(8,128)S(1)}) fusion(pred[512,2048]{0,1:T(8,128)(4,1)S(1)} %iota_compare_fusion, bf16[2,2048,128]{2,1,0:T(8,128)(2,1)} %all-gather.4.cloned.1.call-done, bf16[512,512]{1,0:T(8,128)(2,1)S(1)} %copy-done), kind=kOutput, calls=%fused_computation.2 | convolution fusion | flops 1086322688 | bytes 18882560 | tf_op jit(solution)/shard_map/tkgd,skd->kgts/dot_general | solution.py:220
  51.4 4.2 %fusion.1 = f32[4,512]{1,0:T(4,128)S(1)} fusion(f32[2048,512,4]{1,0,2:T(8,128)S(1)} %get-tuple-element.21, f32[4,512]{1,0:T(4,128)S(1)} %get-tuple-element.20, pred[512,2048]{0,1:T(8,128)(4,1)S(1)} %iota_compare_fusion), kind=kLoop, calls=%fused_computation.3 | loop fusion | flops 20969472 | bytes 17842176 | tf_op jit(solution)/shard_map/reduce_sum | solution.py:228
  55.6 0.0 copy-done.5
  55.6 0.0 copy-start.4
  55.6 4.7 %fusion.12 = (bf16[]{:T(256)}, bf16[4,512,128]{1,2,0:T(8,128)(2,1)S(1)}) fusion(f32[4,512]{1,0:T(4,128)S(1)} %fusion.1, bf16[2,2048,128]{2,1,0:T(8,128)(2,1)S(1)} %copy-done.5, f32[2048,512,4]{1,0,2:T(8,128)S(1)} %get-tuple-element.21, f32[4,512]{1,0:T(4,128)S(1)} %get-tuple-element.20, pred[512,2048]{0,1:T(8,128)(4,1)S(1)} %iota_compare_fusion), kind=kOutput, calls=%fused_computation.17 | convolution fusion | flops 1095761920 | bytes 18890754 | tf_op jit(solution)/shard_map/kgts,skd->kgtd/dot_general | solution.py:229
  60.3 0.7 constant_dynamic-slice_fusion.1
  61.1 0.3 collective-permute-start
  61.4 0.0 copy-done.4
  61.4 0.6 reshape.69
  62.0 20.3 %quant_weight.3.refs_3_ = bf16[512,6144]{1,0:T(8,128)(2,1)} custom-call(f32[1,1]{1,0:T(1,128)} %pmax.22.peak_ref, bf16[512,8192]{1,0:T(8,128)(2,1)} %w_ref.3), custom_call_target="tpu_custom_call" | custom-call | flops 125829120 | bytes 12582912 | tf_op jit(solution)/shard_map/quant_weight/pallas_call | solution.py:61
  82.3 23.2 %pmax.21.refs_0_ = f32[1,1]{1,0:T(1,128)} all-reduce(bf16[1,1]{1,0:T(2,128)(2,1)} %bitcast.21), channel_id=1, replica_groups=mesh['dp'=4,'seq'=4,'tp'=2] {'seq','tp'}, use_global_device_ids=true, to_apply=%region_3.4 | all-reduce | flops 1 | bytes 6 | tf_op jit(solution)/shard_map/pmax | solution.py:268
  105.5 0.0 collective-permute-done.refs_2_
  105.5 0.0 copy-start.2
  105.5 0.0 collective-permute-done.2
  105.5 0.7 broadcast_in_dim.20.refs_7_.refs_8_
  106.2 0.1 copy-done.2
  106.3 8.5 %project.2 = (bf16[256,8192]{1,0:T(8,128)(2,1)}, f32[256,8192]{1,0:T(8,128)}, f32[256,128]{1,0:T(8,128)}, f32[256,128]{1,0:T(8,128)}, f32[256,128]{1,0:T(8,128)}, /*index=5*/f32[8,128]{1,0:T(8,128)}) custom-call(f32[1,1]{1,0:T(1,128)} %pmax.21.refs_0_, bf16[512,256]{1,0:T(8,128)(2,1)} %get-tuple-element.19.refs_1_, bf16[512,256]{1,0:T(8,128)(2,1)} %copy-done.2, ...), custom_call_target="tpu_custom_call" | custom-call | flops 1073741824 | bytes 4194304 | tf_op jit(solution)/shard_map/project/pallas_call | solution.py:132
  114.8 0.0 all-gather.6.cloned.1.call-done
  114.8 0.0 copy-start.1
  114.8 19.5 %project.3 = (bf16[256,8192]{1,0:T(8,128)(2,1)}, f32[256,8192]{1,0:T(8,128)}, f32[256,128]{1,0:T(8,128)}, f32[256,128]{1,0:T(8,128)}, f32[256,128]{1,0:T(8,128)}, /*index=5*/f32[8,128]{1,0:T(8,128)}) custom-call(f32[1,1]{1,0:T(1,128)} %pmax.21.refs_0_, bf16[512,256]{1,0:T(8,128)(2,1)} %get-tuple-element.19.refs_1_, ...), custom_call_target="tpu_custom_call", output_to_operand_aliasing={{0}: (9, {}), {1}: (10, {})} | custom-call | flops 3221225472 | bytes 12582912 | tf_op jit(solution)/shard_map/project/pallas_call | solution.py:132
  134.3 1.2 slice.11
  135.5 12.6 %pmax.23.peak_ref = f32[1,1]{1,0:T(1,128)} all-reduce(f32[1,1]{1,0:T(1,128)} %slice.11), channel_id=1, replica_groups=mesh['dp'=4,'seq'=4,'tp'=2] {'seq','tp'}, use_global_device_ids=true, to_apply=%region_6.7 | all-reduce | flops 1 | bytes 8 | tf_op jit(solution)/shard_map/pmax | solution.py:278
  148.1 20.9 %final_quant.1 = bf16[256,8192]{1,0:T(8,128)(2,1)} custom-call(f32[1,1]{1,0:T(1,128)} %pmax.23.peak_ref, f32[256,8192]{1,0:T(8,128)} %get-tuple-element.16.hid_ref, f32[256,128]{1,0:T(8,128)} %get-tuple-element.17.rstd_ref, f32[1,8192]{1,0:T(1,128)} %bitcast.68), custom_call_target="tpu_custom_call" | custom-call | tf_op jit(solution)/shard_map/final_quant/pallas_call | solution.py:194
  169.1 0.0 copy-done.1
  (1 shorter events, 0.0 us)
Async XLA Ops:
  7.2 40.0 %copy-start = (bf16[512,512]{1,0:T(8,128)(2,1)S(1)}, bf16[512,512]{1,0:T(8,128)(2,1)}, u32[]{:S(2)}) copy-start(bf16[512,512]{1,0:T(8,128)(2,1)} %param.6) | copy-start | bytes 1572868
  7.2 39.9 %all-gather.4.cloned.1.call-start = ((), (), s32[]{:S(2)}) async-start(), calls=%async_computation | async-start | bytes 1310720 | tf_op jit(solution)/shard_map/all_gather | solution.py:243
  9.0 105.8 %all-gather.6.cloned.1.call-start = ((), (), s32[]{:S(2)}) async-start(), calls=%async_computation.1 | async-start | bytes 6684672 | tf_op jit(solution)/shard_map/all_gather | solution.py:255
  25.9 10.2 %collective-permute-start.1 = (bf16[512,384]{1,0:T(8,128)(2,1)}, bf16[512,384]{1,0:T(8,128)(2,1)S(1)}, u32[]{:S(2)}, u32[]{:S(2)}) collective-permute-start(bf16[512,384]{1,0:T(8,128)(2,1)} %quant_weight.4), channel_id=1, source_target_pairs={{0,1},{1,0},{2,3},{3,2},{4,5},{5,4},{6,7},{7,6},{8,9},{9,8},{10,11... | collective-permute-start | bytes 1179656 | tf_op jit(solution)/shard_map/ppermute | solution.py:254
  36.2 0.8 copy-start.3
  44.5 61.0 %collective-permute-start.2 = (bf16[512,2048]{1,0:T(8,128)(2,1)}, bf16[512,2048]{1,0:T(8,128)(2,1)}, u32[]{:S(2)}, u32[]{:S(2)}) collective-permute-start(bf16[512,2048]{1,0:T(8,128)(2,1)} %quant_weight.5.refs_3_), channel_id=1, source_target_pairs={{0,1},{1,0},{2,3},{3,2},{4,5},{5,4},{6,7},{7,6},{8,9},{9,8},{10,11... | collective-permute-start | bytes 6291464 | tf_op jit(solution)/shard_map/ppermute | solution.py:257
  47.1 8.5 %copy-start.5 = (bf16[2,2048,128]{2,1,0:T(8,128)(2,1)S(1)}, bf16[2,2048,128]{2,1,0:T(8,128)(2,1)}, u32[]{:S(2)}) copy-start(bf16[2,2048,128]{2,1,0:T(8,128)(2,1)} %all-gather.4.cloned.1.call-done) | copy-start | bytes 3145732
  55.6 5.8 %copy-start.4 = (bf16[8192]{0:T(1024)(128)(2,1)S(1)}, bf16[8192]{0:T(1024)(128)(2,1)}, u32[]{:S(2)}) copy-start(bf16[8192]{0:T(1024)(128)(2,1)} %param.11) | copy-start | bytes 49156
  61.1 44.4 %collective-permute-start = (bf16[512,256]{1,0:T(8,128)(2,1)S(1)}, bf16[512,256]{1,0:T(8,128)(2,1)S(1)}, u32[]{:S(2)}, u32[]{:S(2)}) collective-permute-start(bf16[512,256]{1,0:T(8,128)(2,1)S(1)} %get-tuple-element.18), channel_id=1, source_target_pairs={{0,1},{1,0},{2,3},{3,2},{4,5},{5,4},{6,7},{7,6},{8,9},{9,8},{10,11... | collective-permute-start | bytes 786440 | tf_op jit(solution)/shard_map/ppermute | solution.py:267
  105.5 0.8 copy-start.2
  114.8 54.3 %copy-start.1 = (bf16[512,512]{1,0:T(8,128)(2,1)S(1)}, bf16[512,512]{1,0:T(8,128)(2,1)}, u32[]{:S(2)}) copy-start(bf16[512,512]{1,0:T(8,128)(2,1)} %param.6) | copy-start | bytes 1572868
Sparse Core Ops, SparseCore 0:
  9.6 19.4 all-gather.3
  37.1 62.9 all-gather.5
where the time goes:
time: 178 us; the launch traced here: 176 us
  Pallas kernels  80.2 us (45%)
  blocking collectives  42.4 us (24%)
  between operations  14.1 us (8%)
  other arithmetic  12.5 us (7%)
  matrix products  8.99 us (5%)
  waiting for transfers between devices  8.28 us (5%)
  local copies, waits for them, and re-layouts  5.26 us (3%)
  starting transfers between devices  4.18 us (2%)
    pallas_call x3, Pallas kernels, quant_weight(): pl.pallas_call(functools.partial(quant_kernel, unroll=4), grid=(cols // w...  31.3 us
    pallas_call x2, Pallas kernels, project(): pl.pallas_call(functools.partial(project_kernel, n_tp=n_tp, n_feat=n_feat...  28 us
    pmax x1, blocking collectives, local(): act_peak = lax.pmax(act_top, ('seq', 'tp')).reshape(1, 1)  23.2 us
    pallas_call x1, Pallas kernels, final_quant(): pl.pallas_call(final_kernel, grid=(tokens // rows, d // width), in_specs=...  20.9 us
    pmax x1, blocking collectives, local(): norm_peak = lax.pmax(top[0, 0], ('seq', 'tp')).reshape(1, 1)  12.6 us
    ppermute x1, waiting for transfers between devices, local(): lax.ppermute(slab_q, 'tp', ring)  8.2 us
    pmax x1, blocking collectives, local(): weight_peak = lax.pmax(weight_top, 'tp').reshape(1, 1)  6.54 us
    reduce_max x1, other arithmetic, local(): weight_top = jnp.max(jnp.abs(out_weight)).astype(jnp.float32)  5.13 us
  transfers between devices with their start and end apart: 5, of which 1 were waited for; matrix products, arithmetic and copies ran while one was open for 13% of the time, Pallas kernels for 23%

commit v1 on v0

--- a/solution.py
+++ b/solution.py
@@ -12,6 +12,9 @@
 softness = 0.9
 scale_floor = 256.0
 neg_large = -1e30
+LANES = 128
+AHEAD = 3
+OWN_FIRST = 4
 ROUND_BIG = 12582912.0
 Q_COEFFS = (0.8999997814, -0.5804296733, 0.1500389216, -0.0212977078, 0.0016888914)
 
@@ -233,7 +236,7 @@
     return attended.transpose(0, 1, 3, 2).reshape(-1, token_count)
 
 
-def local(queries, keys, values, out_weight, residual, norm_gain):
+def general(queries, keys, values, out_weight, residual, norm_gain):
     token_count = queries.shape[0]
     n_tp = lax.axis_size("tp")
     tp_rank = lax.axis_index("tp")
@@ -280,6 +283,562 @@
     return (new_residual, next_input)
 
 
+def quant_tile(src, dst, inv, tensor_scale):
+    rows = src.shape[0]
+    step = 128 if rows % 128 == 0 else BLOCK
+    for lo in range(0, rows, step):
+        x = src[lo : lo + step, :].astype(jnp.float32).reshape(step // BLOCK, BLOCK, LANES)
+        block_max = jnp.max(jnp.abs(x), axis=1, keepdims=True)
+        scale = jnp.maximum(block_max * inv, scale_floor).astype(jnp.bfloat16)
+        spacing = scale.astype(jnp.float32) * tensor_scale
+        payload = soft_grid(x * (1.0 / spacing)).astype(jnp.bfloat16).astype(jnp.float32)
+        dst[lo : lo + step, :] = (payload * spacing).reshape(step, LANES).astype(jnp.bfloat16)
+
+
+def scales_of(top):
+    tensor_scale = top / (6.0 * 448.0)
+    return 1.0 / (6.0 * tensor_scale), tensor_scale
+
+
+def lane_block_max(m):
+    for s in (1, 2, 4, 8):
+        m = jnp.maximum(m, pltpu.roll(m, s, 1))
+    return m
+
+
+def spread_matrix():
+    src = lax.broadcasted_iota(jnp.int32, (LANES, LANES), 0)
+    dst = lax.broadcasted_iota(jnp.int32, (LANES, LANES), 1)
+    return jnp.where(src == (dst // BLOCK) * BLOCK + BLOCK - 1, 1.0, 0.0).astype(jnp.bfloat16)
+
+
+def fused_kernel(
+    q_hbm, k_hbm, v_hbm, w_hbm, res_hbm, gain_ref,
+    hid_hbm, rstd_ref, top_ref,
+    q_buf, kv_buf, raw_own, raw_peer, w_own, w_peer, res_buf, hid_buf,
+    act_full, act_peer, act_q, square_sum, row_top, peaks,
+    part_own, part_peer,
+    local_sem, load_sem, recv_sem, x_sem, y_sem, z_sem,
+    kv_send, kv_recv, peak_send, peak_recv, act_sem,
+    own_send, own_recv, peer_send, peer_recv, out_sem,
+    *, features,
+):
+    tokens = k_hbm.shape[0]
+    heads = q_hbm.shape[1] // HEAD_SIZE
+    share = res_hbm.shape[0]
+    n_feat = heads * HEAD_SIZE
+    tiles = raw_own.shape[0]
+    group = tiles // 4
+    pairs = tiles // 2
+    group_pairs = group // 2
+    relay_x = group // 4
+    relay_y = group // 4
+    dp, seq, tp = lax.axis_index("dp"), lax.axis_index("seq"), lax.axis_index("tp")
+    core, y = seq % 2, seq // 2
+    zz = dp % 2
+    x_dev = {"dp": dp, "seq": seq, "tp": 1 - tp}
+    y_dev = {"dp": dp, "seq": (1 - y) * 2 + core, "tp": tp}
+    z_dev = {"dp": dp + 1 - 2 * zz, "seq": seq, "tp": tp}
+    s_dev = {"dp": dp, "seq": y * 2 + 1 - core, "tp": tp}
+
+    def remote(src, dst, send, recv, dev):
+        return pltpu.make_async_remote_copy(
+            src_ref=src, dst_ref=dst, send_sem=send, recv_sem=recv,
+            device_id=dev, device_id_type=pl.DeviceIdType.MESH,
+        )
+
+    g_mine, g_y = y + 2 * zz, (1 - y) + 2 * zz
+    g_z, g_d = y + 2 * (1 - zz), (1 - y) + 2 * (1 - zz)
+    x_count = group + relay_x
+    y_count = group + relay_y
+    z_count = group + (group - relay_x - relay_y)
+
+    def x_send(i):
+        late = i // group
+        j = (1 - late) * (g_mine * group + i) + late * (g_d * group + i - group)
+        return remote(raw_own.at[j], raw_peer.at[j], x_sem.at[i], recv_sem.at[j], x_dev)
+
+    def y_send(i, j):
+        return remote(raw_peer.at[j], raw_peer.at[j], y_sem.at[i], recv_sem.at[j], y_dev)
+
+    def z_send(i, j):
+        return remote(raw_peer.at[j], raw_peer.at[j], z_sem.at[i], recv_sem.at[j], z_dev)
+
+    def wait_tile(j):
+        remote(raw_peer.at[j], raw_peer.at[j], x_sem.at[0], recv_sem.at[j], x_dev).wait_recv()
+
+    def forward(i):
+        j = g_mine * group + i
+        wait_tile(j)
+        y_send(i, j).start()
+        z_send(i, j).start()
+
+        @pl.when(i + AHEAD < x_count)
+        def _():
+            x_send(i + AHEAD).start()
+
+    col0 = core * tiles
+
+    def load(j):
+        cols = pl.ds(pl.multiple_of((col0 + j) * LANES, LANES), LANES)
+        return pltpu.make_async_copy(w_hbm.at[:, cols], raw_own.at[j], load_sem.at[j])
+
+    k_load = pltpu.make_async_copy(k_hbm, kv_buf.at[seq, 0], local_sem.at[0])
+    v_load = pltpu.make_async_copy(v_hbm, kv_buf.at[seq, 1], local_sem.at[1])
+    res_load = pltpu.make_async_copy(res_hbm, res_buf, local_sem.at[2])
+    q_loads = [
+        pltpu.make_async_copy(
+            q_hbm.at[:, h * HEAD_SIZE : (h + 1) * HEAD_SIZE], q_buf.at[h], local_sem.at[3 + h]
+        )
+        for h in range(heads)
+    ]
+
+    def load_order(n):
+        return lax.rem(g_mine * group + n, tiles)
+
+    def start_load(n, c):
+        load(load_order(n)).start()
+        return c
+
+    k_load.start()
+    v_load.start()
+    lax.fori_loop(0, tiles, start_load, 0)
+    for c in q_loads:
+        c.start()
+    res_load.start()
+
+    barrier = pltpu.get_barrier_semaphore()
+    team = []
+    for ds in range(4):
+        for dt in range(2):
+            if ds or dt:
+                team.append((ds, dt))
+    for ds, dt in team:
+        dev = {"dp": dp, "seq": lax.rem(seq + ds, 4), "tp": lax.rem(tp + dt, 2)}
+        pl.semaphore_signal(barrier, inc=1, device_id=dev, device_id_type=pl.DeviceIdType.MESH)
+    pl.semaphore_signal(barrier, inc=1, device_id=z_dev, device_id_type=pl.DeviceIdType.MESH)
+    pl.semaphore_wait(barrier, len(team) + 1)
+
+    k_load.wait()
+    v_load.wait()
+    other = y * 2 + 1 - core
+    far = (1 - y) * 2 + core
+    far_other = (1 - y) * 2 + 1 - core
+    kv_y = remote(kv_buf.at[seq], kv_buf.at[seq], kv_send.at[0], kv_recv.at[seq], y_dev)
+    kv_s = remote(kv_buf.at[seq], kv_buf.at[seq], kv_send.at[1], kv_recv.at[seq], s_dev)
+    kv_f = remote(kv_buf.at[far], kv_buf.at[far], kv_send.at[2], kv_recv.at[far], s_dev)
+    kv_y.start()
+    kv_s.start()
+
+    def wait_load(n, c):
+        load(load_order(n)).wait()
+        return c
+
+    lax.fori_loop(0, group, wait_load, 0)
+    for i in range(AHEAD):
+        x_send(i).start()
+    lax.fori_loop(group, tiles, wait_load, 0)
+
+    def peak_exchange(kind, value, members):
+        me = seq * 2 + tp
+        peaks[kind, me] = value
+        sends = []
+        for ds, dt in members:
+            ps = ds(seq) if callable(ds) else lax.rem(seq + ds, 4)
+            pt = lax.rem(tp + dt, 2)
+            dev = {"dp": dp, "seq": ps, "tp": pt}
+            n = len(sends)
+            out = remote(
+                peaks.at[kind, me], peaks.at[kind, me], peak_send.at[kind, n],
+                peak_recv.at[kind, me], dev,
+            )
+            out.start()
+            sends.append((out, ps * 2 + pt))
+
+        def finish():
+            top = value
+            for out, them in sends:
+                remote(
+                    peaks.at[kind, them], peaks.at[kind, them], peak_send.at[kind, 0],
+                    peak_recv.at[kind, them], x_dev,
+                ).wait_recv()
+                top = jnp.maximum(top, peaks[kind, them])
+            return top
+
+        return finish, [out for out, _ in sends]
+
+    def tile_top(j, m):
+        x = jnp.abs(raw_own[j]).reshape(-1, 4 * BLOCK, LANES)
+        return jnp.maximum(m, jnp.max(x, axis=0))
+
+    w_top = lax.fori_loop(0, tiles, tile_top, jnp.zeros((4 * BLOCK, LANES), jnp.bfloat16))
+    w_top = jnp.full((8, LANES), jnp.max(w_top.astype(jnp.float32)), jnp.float32)
+
+    def sib(s):
+        return (s // 2) * 2 + 1 - s % 2
+
+    finish_w, w_sends = peak_exchange(0, w_top, [(sib, 0), (0, 1), (sib, 1)])
+
+    remote(kv_buf.at[far], kv_buf.at[far], kv_send.at[0], kv_recv.at[far], y_dev).wait_recv()
+    kv_f.start()
+
+    w_inv, w_scale = scales_of(finish_w()[0:1, :])
+
+    def own_copy(p):
+        sl = pl.ds(col0 + 2 * p, 2)
+        return remote(w_own.at[sl], w_own.at[sl], own_send.at[p], own_recv.at[p], s_dev)
+
+    def own_pair(p, c):
+        for t in range(2):
+            quant_tile(raw_own.at[2 * p + t], w_own.at[col0 + 2 * p + t], w_inv, w_scale)
+        own_copy(p).start()
+        return c
+
+    lax.fori_loop(0, OWN_FIRST, own_pair, 0)
+    forward(0)
+
+    for c in q_loads:
+        c.wait()
+    for slot in (other, far_other):
+        remote(kv_buf.at[slot], kv_buf.at[slot], kv_send.at[0], kv_recv.at[slot], s_dev).wait_recv()
+
+    rate = HEAD_SIZE ** (-0.5)
+
+    def scores_of(q, b):
+        return lax.dot_general(
+            q, kv_buf[b, 0], (((1,), (1,)), ((), ())), preferred_element_type=jnp.float32
+        )
+
+    def attend_tile(first, h):
+        q = q_buf[h, pl.ds(first, share), :]
+        s = scores_of(q, seq)
+        row = lax.broadcasted_iota(jnp.int32, (share, tokens), 0) + first
+        col = lax.broadcasted_iota(jnp.int32, (share, tokens), 1)
+        s = jnp.where(row >= col, s, neg_large)
+        top = jnp.max(s, axis=1, keepdims=True)
+        p = jnp.exp((s - top) * rate)
+        total = jnp.sum(p, axis=1, keepdims=True)
+        acc = jnp.dot(p.astype(jnp.bfloat16), kv_buf[seq, 1], preferred_element_type=jnp.float32)
+
+        def body(b, carry):
+            top, total, acc = carry
+            s = scores_of(q, b)
+            new = jnp.maximum(top, jnp.max(s, axis=1, keepdims=True))
+            fix = jnp.exp((top - new) * rate)
+            p = jnp.exp((s - new) * rate)
+            total = total * fix + jnp.sum(p, axis=1, keepdims=True)
+            acc = acc * fix + jnp.dot(
+                p.astype(jnp.bfloat16), kv_buf[b, 1], preferred_element_type=jnp.float32
+            )
+            return new, total, acc
+
+        top, total, acc = lax.fori_loop(0, seq, body, (top, total, acc))
+        out = (acc / total).astype(jnp.bfloat16)
+        act_full[h, pl.ds(first, share), :] = out
+        return jnp.max(jnp.abs(out.astype(jnp.float32)), axis=0, keepdims=True)
+
+    theirs = pl.multiple_of((1 - tp) * share, share)
+    mine = pl.multiple_of(tp * share, share)
+    a_top = jnp.zeros((1, LANES), jnp.float32)
+
+    def att_loop(first):
+        def body(h, m):
+            return jnp.maximum(m, attend_tile(first, h))
+
+        return body
+
+    a_top = lax.fori_loop(0, heads, att_loop(theirs), a_top)
+    act_copy = remote(
+        act_full.at[:, pl.ds(theirs, share), :], act_peer, act_sem.at[0], act_sem.at[1], x_dev
+    )
+    act_copy.start()
+    forward(1)
+    forward(2)
+    a_top = lax.fori_loop(0, heads, att_loop(mine), a_top)
+    a_top = jnp.full((8, LANES), jnp.max(a_top), jnp.float32)
+    finish_a, a_sends = peak_exchange(1, a_top, team)
+
+    forward(3)
+    third = (pairs - OWN_FIRST) // 3
+    lax.fori_loop(OWN_FIRST, OWN_FIRST + third, own_pair, 0)
+    forward(4)
+    lax.fori_loop(OWN_FIRST + third, OWN_FIRST + 2 * third, own_pair, 0)
+    forward(5)
+    lax.fori_loop(OWN_FIRST + 2 * third, pairs, own_pair, 0)
+    for i in range(6, group):
+        forward(i)
+
+    a_inv, a_scale = scales_of(finish_a()[0:1, :])
+    act_copy.wait_recv()
+    spread = spread_matrix()
+    for k in range(2):
+        for h in range(heads):
+            for lo in range(0, share, 64):
+                if k == 0:
+                    x = act_full[h, pl.ds(mine + lo, 64), :].astype(jnp.float32)
+                else:
+                    x = act_peer[h, lo : lo + 64, :].astype(jnp.float32)
+                m = lane_block_max(jnp.abs(x))
+                narrow = jnp.maximum(m * a_inv, scale_floor).astype(jnp.bfloat16)
+                spacing = jnp.dot(narrow, spread, preferred_element_type=jnp.float32) * a_scale
+                payload = soft_grid(x * (1.0 / spacing)).astype(jnp.bfloat16).astype(jnp.float32)
+                act_q[k, lo : lo + 64, h * HEAD_SIZE : (h + 1) * HEAD_SIZE] = (
+                    payload * spacing
+                ).astype(jnp.bfloat16)
+
+    square_sum[...] = jnp.zeros_like(square_sum)
+    row_top[...] = jnp.zeros_like(row_top)
+
+    def local_pair(p):
+        late = p // (3 * group_pairs)
+        sel = lax.rem(p, 3)
+        fy = late + (1 - late) * (sel % 2)
+        fz = late + (1 - late) * (sel // 2)
+        g = lax.rem(y + fy, 2) + 2 * lax.rem(zz + fz, 2)
+        i = (1 - late) * (p // 3) + late * (p - 3 * group_pairs)
+        return g * group_pairs + i, late, sel, i
+
+    def peer_copy(lp):
+        sl = pl.ds(col0 + 2 * lp, 2)
+        return remote(w_peer.at[sl], w_peer.at[sl], peer_send.at[lp], peer_recv.at[lp], s_dev)
+
+    def out_copy(n):
+        cols = pl.ds(pl.multiple_of(2 * n * LANES, 2 * LANES), 2 * LANES)
+        return pltpu.make_async_copy(hid_buf.at[:, cols], hid_hbm.at[:, cols], out_sem.at[n])
+
+    def project_pair(n):
+        cols = pl.ds(pl.multiple_of(2 * n * LANES, 2 * LANES), 2 * LANES)
+        a = jnp.concatenate([w_own[2 * n], w_own[2 * n + 1]], axis=1)
+        b = jnp.concatenate([w_peer[2 * n], w_peer[2 * n + 1]], axis=1)
+        part_own[...] = jnp.dot(act_q[0], a, preferred_element_type=jnp.float32)
+        part_peer[...] = jnp.dot(act_q[1], b, preferred_element_type=jnp.float32)
+        gain = gain_ref[:, cols]
+        for lo in range(0, share, 32):
+            p0 = part_own[lo : lo + 32, :].astype(jnp.bfloat16).astype(jnp.float32)
+            p1 = part_peer[lo : lo + 32, :].astype(jnp.bfloat16).astype(jnp.float32)
+            h = res_buf[lo : lo + 32, cols].astype(jnp.float32) + (p0 + p1)
+            hid_buf[lo : lo + 32, cols] = h
+            s = jnp.abs(h * gain)
+            h = h * h
+            square_sum[lo : lo + 32, :] += h[:, :LANES] + h[:, LANES:]
+            row_top[lo : lo + 32, :] = jnp.maximum(
+                row_top[lo : lo + 32, :], jnp.maximum(s[:, :LANES], s[:, LANES:])
+            )
+        out_copy(n).start()
+
+    other0 = (1 - core) * tiles
+
+    def sibling_pair(lp):
+        sl = pl.ds(other0 + 2 * lp, 2)
+        remote(w_own.at[sl], w_own.at[sl], own_send.at[0], own_recv.at[lp], s_dev).wait_recv()
+        remote(w_peer.at[sl], w_peer.at[sl], peer_send.at[0], peer_recv.at[lp], s_dev).wait_recv()
+        project_pair(other0 // 2 + lp)
+
+    res_load.wait()
+
+    def step(p, c):
+        lp, late, sel, i = local_pair(p)
+
+        @pl.when(late + sel > 0)
+        def _():
+            wait_tile(2 * lp)
+            wait_tile(2 * lp + 1)
+
+        @pl.when((1 - late) * sel * (sel % 2) * (2 * i // (relay_x + relay_y)) > 0)
+        def _():
+            for t in range(2):
+                n = 2 * i + t - relay_x - relay_y
+                z_send(group + n, 2 * lp + t).start()
+
+        for lo in range(relay_x // 2, (relay_x + relay_y) // 2):
+            @pl.when((1 - late) * (sel // 2) * (1 - (i - lo) * (i - lo)) > 0)
+            def _():
+                for t in range(2):
+                    n = 2 * (lo - relay_x // 2) + t
+                    y_send(group + n, 2 * lp + t).start()
+
+        for t in range(2):
+            quant_tile(raw_peer.at[2 * lp + t], w_peer.at[col0 + 2 * lp + t], w_inv, w_scale)
+        peer_copy(lp).start()
+        project_pair(col0 // 2 + lp)
+
+        @pl.when(p > 0)
+        def _():
+            sibling_pair(local_pair(p - 1)[0])
+
+        return c
+
+    lax.fori_loop(0, pairs, step, 0)
+    sibling_pair(local_pair(pairs - 1)[0])
+
+    mean_square = jnp.sum(square_sum[...], axis=1, keepdims=True) / features
+    rstd = lax.rsqrt(mean_square + 1e-05)
+    rstd_ref[...] = jnp.broadcast_to(rstd, rstd_ref.shape)
+    n_top = jnp.max(jnp.max(row_top[...], axis=1, keepdims=True) * rstd)
+    finish_n, n_sends = peak_exchange(2, jnp.full((8, LANES), n_top, jnp.float32), team)
+
+    kv_y.wait_send()
+    kv_s.wait_send()
+    kv_f.wait_send()
+    act_copy.wait_send()
+    for c in w_sends + a_sends:
+        c.wait_send()
+
+    def drain(n, c):
+        own_copy(n).wait_send()
+        peer_copy(n).wait_send()
+        out_copy(n).wait()
+        out_copy(n + pairs).wait()
+        return c
+
+    lax.fori_loop(0, pairs, drain, 0)
+
+    def drain_links(i, c):
+        remote(raw_own.at[0], raw_peer.at[0], x_sem.at[i], recv_sem.at[0], x_dev).wait_send()
+        y_send(i, 0).wait_send()
+        return c
+
+    lax.fori_loop(0, x_count, drain_links, 0)
+
+    def drain_z(i, c):
+        z_send(i, 0).wait_send()
+        return c
+
+    lax.fori_loop(0, z_count, drain_z, 0)
+    top_ref[...] = finish_n()
+    for c in n_sends:
+        c.wait_send()
+
+
+def fused(queries, keys, values, out_weight, residual, gain):
+    tokens, n_feat = queries.shape
+    share, d = residual.shape
+    heads = n_feat // HEAD_SIZE
+    tiles = d // LANES // 2
+    pairs = tiles // 2
+    group = tiles // 4
+    any_spec = pl.BlockSpec(memory_space=pl.ANY)
+    vmem = pl.BlockSpec(memory_space=pltpu.VMEM)
+    dma = pltpu.SemaphoreType.DMA
+    bf16, f32 = jnp.bfloat16, jnp.float32
+    rows = out_weight.shape[0]
+    return pl.pallas_call(
+        functools.partial(fused_kernel, features=d),
+        in_specs=[any_spec] * 5 + [vmem],
+        out_specs=[any_spec, vmem, vmem],
+        out_shape=[
+            jax.ShapeDtypeStruct((share, d), f32),
+            jax.ShapeDtypeStruct((share, LANES), f32),
+            jax.ShapeDtypeStruct((8, LANES), f32),
+        ],
+        scratch_shapes=[
+            pltpu.VMEM((heads, tokens, HEAD_SIZE), bf16),
+            pltpu.VMEM((4, 2, tokens, HEAD_SIZE), bf16),
+            pltpu.VMEM((tiles, rows, LANES), bf16),
+            pltpu.VMEM((tiles, rows, LANES), bf16),
+            pltpu.VMEM((2 * tiles, rows, LANES), bf16),
+            pltpu.VMEM((2 * tiles, rows, LANES), bf16),
+            pltpu.VMEM((share, d), bf16),
+            pltpu.VMEM((share, d), f32),
+            pltpu.VMEM((heads, tokens, HEAD_SIZE), bf16),
+            pltpu.VMEM((heads, share, HEAD_SIZE), bf16),
+            pltpu.VMEM((2, share, n_feat), bf16),
+            pltpu.VMEM((share, LANES), f32),
+            pltpu.VMEM((share, LANES), f32),
+            pltpu.VMEM((3, 8, 8, LANES), f32),
+            pltpu.VMEM((share, 2 * LANES), f32),
+            pltpu.VMEM((share, 2 * LANES), f32),
+            dma((3 + heads,)),
+            dma((tiles,)),
+            dma((tiles,)),
+            dma((group + group // 4,)),
+            dma((group + group // 4,)),
+            dma((2 * group - 2 * (group // 4),)),
+            dma((3,)),
+            dma((4,)),
+            dma((3, 7)),
+            dma((3, 8)),
+            dma((2,)),
+            dma((pairs,)),
+            dma((pairs,)),
+            dma((pairs,)),
+            dma((pairs,)),
+            dma((2 * pairs,)),
+        ],
+        compiler_params=pltpu.CompilerParams(
+            collective_id=0, has_side_effects=True, vmem_limit_bytes=60 * 1024 * 1024
+        ),
+        name="fused",
+    )(queries, keys, values, out_weight, residual, gain)
+
+
+def final_fast_kernel(top_ref, hid_ref, rstd_ref, gain_ref, new_ref, out_ref, narrow, wide):
+    rows, cols = hid_ref.shape
+    inv, tensor_scale = scales_of(top_ref[0:1, :])
+    spread = spread_matrix()
+    rstd = rstd_ref[...]
+    pieces = cols // LANES
+    for i in range(pieces):
+        sl = slice(i * LANES, (i + 1) * LANES)
+        h = hid_ref[:, sl]
+        new_ref[:, sl] = h.astype(jnp.bfloat16)
+        m = lane_block_max(jnp.abs(h * rstd * gain_ref[:, sl]))
+        narrow[i * rows : (i + 1) * rows, :] = jnp.maximum(m * inv, scale_floor).astype(jnp.bfloat16)
+    wide[...] = jnp.dot(narrow[...], spread, preferred_element_type=jnp.float32)
+    for i in range(pieces):
+        sl = slice(i * LANES, (i + 1) * LANES)
+        x = hid_ref[:, sl] * rstd * gain_ref[:, sl]
+        spacing = wide[i * rows : (i + 1) * rows, :] * tensor_scale
+        payload = soft_grid(x * pl.reciprocal(spacing)).astype(jnp.bfloat16).astype(jnp.float32)
+        out_ref[:, sl] = (payload * spacing).astype(jnp.bfloat16)
+
+
+def final_fast(top, hidden, rstd, gain):
+    tokens, d = hidden.shape
+    width, rows = 2048, 64
+    column = pl.BlockSpec((rows, width), lambda i, j: (i, j))
+    return pl.pallas_call(
+        final_fast_kernel,
+        grid=(tokens // rows, d // width),
+        in_specs=[
+            pl.BlockSpec((8, LANES), lambda i, j: (0, 0)),
+            column,
+            pl.BlockSpec((rows, LANES), lambda i, j: (i, 0)),
+            pl.BlockSpec((1, width), lambda i, j: (0, j)),
+        ],
+        out_specs=[column, column],
+        out_shape=[jax.ShapeDtypeStruct((tokens, d), jnp.bfloat16)] * 2,
+        scratch_shapes=[
+            pltpu.VMEM((rows * width // LANES, LANES), jnp.bfloat16),
+            pltpu.VMEM((rows * width // LANES, LANES), jnp.float32),
+        ],
+        name="final_fast",
+    )(top, hidden, rstd, gain)
+
+
+def fits_fused(queries, keys, out_weight, residual):
+    sizes = {a: lax.axis_size(a) for a in ("dp", "seq", "tp")}
+    return (
+        sizes["tp"] == 2
+        and sizes["seq"] == 4
+        and sizes["dp"] % 2 == 0
+        and keys.shape[1] == HEAD_SIZE
+        and out_weight.shape[1] % (64 * LANES) == 0
+        and out_weight.shape[0] == queries.shape[1]
+        and out_weight.shape[0] % LANES == 0
+        and residual.shape[0] * 2 == queries.shape[0]
+        and residual.shape[0] % 64 == 0
+    )
+
+
+def local(queries, keys, values, out_weight, residual, norm_gain):
+    if not fits_fused(queries, keys, out_weight, residual):
+        return general(queries, keys, values, out_weight, residual, norm_gain)
+    gain = norm_gain.astype(jnp.float32).reshape(1, -1)
+    hidden, rstd, top = fused(queries, keys, values, out_weight, residual, gain)
+    return tuple(final_fast(top, hidden, rstd, gain))
+
+
 def solution(mesh):
     in_specs = (
         P(("dp", "seq"), "tp"),

time: 178 us -> 101 us (0.57); the launches traced: 176 us -> 101 us
  blocking collectives: 42.4 us -> 0 us
  Pallas kernels: 80.2 us -> 98.8 us
  between operations: 14.1 us -> 0.64 us
  other arithmetic: 12.5 us -> 1.32 us
  matrix products: 8.99 us -> 0 us
  waiting for transfers between devices: 8.28 us -> 0 us
  local copies, waits for them, and re-layouts: 5.26 us -> 0 us
  starting transfers between devices: 4.18 us -> 0 us
    pmax x3 -> x0, blocking collectives: 42.4 us -> none  [the longest x1 23.2 us: local(): act_peak = lax.pmax(act_top, ('seq', 'tp')).reshape(1, 1)]
    pallas_call x6 -> x2, Pallas kernels: 80.2 us -> 98.8 us  [the longest x1 78.5 us: fused(): pl.pallas_call(functools.partial(fused_kernel, features=d), in_specs=[any...]
    dot_general x2 -> x0, matrix products: 8.99 us -> none  [the longest x1 4.71 us: attend(): jnp.einsum('kgts,skd->kgtd', weights.astype(jnp.bfloat16), v, preferred_e...]
    ppermute x3 -> x0, waiting for transfers between devices: 8.2 us -> none  [the longest x1 8.2 us: local(): lax.ppermute(slab_q, 'tp', ring)]
    reduce_max x1 -> x0, other arithmetic: 5.13 us -> none  [local(): weight_top = jnp.max(jnp.abs(out_weight)).astype(jnp.float32)]
    reduce_sum x1 -> x0, other arithmetic: 4.18 us -> none  [attend(): total = jnp.sum(weights, axis=3)]
    ppermute x3 -> x0, starting transfers between devices: 4.1 us -> none  [the longest x1 2.04 us: local(): lax.ppermute(slab_q, 'tp', ring)]
    dynamic_slice x2 -> x0, local copies, waits for them, and re-layouts: 2.52 us -> none  [the longest x1 1.78 us: local(): lax.dynamic_slice_in_dim(out_weight, slab_id * gather_w, gather_w, axis=1)]
  transfers between devices with their start and end apart: 5 -> 0, of which waited for: 1 -> 0; matrix products, arithmetic and copies ran while one was open for 13% -> 0% of each run, Pallas kernels for 23% -> 0%
where the time goes in v1:
time: 101 us
  Pallas kernels  98.8 us (98%)
  other arithmetic  1.32 us (1%)
    pallas_call x1, Pallas kernels, fused(): pl.pallas_call(functools.partial(fused_kernel, features=d), in_specs=[any...  78.5 us
    pallas_call x1, Pallas kernels, final_fast(): pl.pallas_call(final_fast_kernel, grid=(tokens // rows, d // width), in_s...  20.3 us

profile of v1, /device:TPU:0, one launch (start us, length us, event | category | flops | bytes accessed | tf_op | source)
XLA Modules:
  0.0 100.7 jit_solution(5957952217152033676)
XLA Ops:
  0.6 1.3 %reshape.11 = f32[8192]{0:T(1024)} convert(bf16[8192]{0:T(1024)(128)(2,1)} %param.11) | non-fusion elementwise | flops 8192 | bytes 49152 | tf_op jit(solution)/shard_map/reshape | solution.py:837
  2.0 78.5 %fused.1 = (f32[256,8192]{1,0:T(8,128)}, f32[256,128]{1,0:T(8,128)}, f32[8,128]{1,0:T(8,128)}) custom-call(bf16[512,512]{1,0:T(8,128)(2,1)} %q_hbm.1, bf16[512,128]{1,0:T(8,128)(2,1)} %k_hbm.1, bf16[512,128]{1,0:T(8,128)(2,1)} %v_hbm.1, bf16[512,8192]{1,0:T(8,128)(2,1)} %w_hbm.1, bf16[256,8192]{1,0:T(8,128)(2,1)} %res_hbm.1, f32[1,8192]{1,0:T(1,128)} %bitcast.1), custom_call_target="tpu_custom_call" | custom-call | tf_op jit(solution)/shard_map/fused/pallas_call | solution.py:725
  80.5 20.3 %final_fast.1 = (bf16[256,8192]{1,0:T(8,128)(2,1)}, bf16[256,8192]{1,0:T(8,128)(2,1)}) custom-call(f32[8,128]{1,0:T(8,128)} %get-tuple-element.5.top_ref, f32[256,8192]{1,0:T(8,128)} %get-tuple-element.6.hid_ref, f32[256,128]{1,0:T(8,128)} %get-tuple-element.7.rstd_ref, f32[1,8192]{1,0:T(1,128)} %bitcast.2), custom_call_target="tpu_custom_call" | custom-call | tf_op jit(solution)/shard_map/final_fast/pallas_call | solution.py:800

commit v2 on v1

--- a/solution.py
+++ b/solution.py
@@ -2,6 +2,7 @@
 
 import jax
 import jax.numpy as jnp
+import numpy as np
 from jax import lax
 from jax.experimental import pallas as pl
 from jax.experimental.pallas import tpu as pltpu
@@ -13,15 +14,14 @@
 scale_floor = 256.0
 neg_large = -1e30
 LANES = 128
-AHEAD = 3
-OWN_FIRST = 4
-ROUND_BIG = 12582912.0
+AHEAD = 2
+RAW = 2
+ROUND_BIG = 25165824.0
 Q_COEFFS = (0.8999997814, -0.5804296733, 0.1500389216, -0.0212977078, 0.0016888914)
 
 
 def soft_grid(u):
-    turns = (u * 0.5 + ROUND_BIG) - ROUND_BIG
-    t = u - (turns + turns)
+    t = u - ((u + ROUND_BIG) - ROUND_BIG)
     z = t * t
     q = jnp.float32(Q_COEFFS[-1])
     for c in Q_COEFFS[-2::-1]:
@@ -314,10 +314,9 @@
 
 def fused_kernel(
     q_hbm, k_hbm, v_hbm, w_hbm, res_hbm, gain_ref,
-    hid_hbm, rstd_ref, top_ref,
+    hid_hbm, rstd_ref, top_ref, bm_ref,
     q_buf, kv_buf, raw_own, raw_peer, w_own, w_peer, res_buf, hid_buf,
-    act_full, act_peer, act_q, square_sum, row_top, peaks,
-    part_own, part_peer,
+    act_full, act_peer, act_q, square_sum, peaks,
     local_sem, load_sem, recv_sem, x_sem, y_sem, z_sem,
     kv_send, kv_recv, peak_send, peak_recv, act_sem,
     own_send, own_recv, peer_send, peer_recv, out_sem,
@@ -331,8 +330,8 @@
     group = tiles // 4
     pairs = tiles // 2
     group_pairs = group // 2
-    relay_x = group // 4
-    relay_y = group // 4
+    direct = group // 4
+    relays = group - direct
     dp, seq, tp = lax.axis_index("dp"), lax.axis_index("seq"), lax.axis_index("tp")
     core, y = seq % 2, seq // 2
     zz = dp % 2
@@ -349,20 +348,24 @@
 
     g_mine, g_y = y + 2 * zz, (1 - y) + 2 * zz
     g_z, g_d = y + 2 * (1 - zz), (1 - y) + 2 * (1 - zz)
-    x_count = group + relay_x
-    y_count = group + relay_y
-    z_count = group + (group - relay_x - relay_y)
+    x_count = group + direct
+    y_count = group + relays // 2
+
+    col0 = core * tiles
+
+    def tile_of(j, raw):
+        return raw_peer.at[j] if raw else w_peer.at[col0 + j]
 
     def x_send(i):
-        late = i // group
-        j = (1 - late) * (g_mine * group + i) + late * (g_d * group + i - group)
-        return remote(raw_own.at[j], raw_peer.at[j], x_sem.at[i], recv_sem.at[j], x_dev)
-
-    def y_send(i, j):
-        return remote(raw_peer.at[j], raw_peer.at[j], y_sem.at[i], recv_sem.at[j], y_dev)
-
-    def z_send(i, j):
-        return remote(raw_peer.at[j], raw_peer.at[j], z_sem.at[i], recv_sem.at[j], z_dev)
+        j = g_mine * group + i if i < group else g_d * group + relays + i - group
+        src = raw_own.at[j] if i < RAW else w_own.at[col0 + j]
+        return remote(src, tile_of(j, i < RAW), x_sem.at[i], recv_sem.at[j], x_dev)
+
+    def y_send(i, j, raw=False):
+        return remote(tile_of(j, raw), tile_of(j, raw), y_sem.at[i], recv_sem.at[j], y_dev)
+
+    def z_send(i, j, raw=False):
+        return remote(tile_of(j, raw), tile_of(j, raw), z_sem.at[i], recv_sem.at[j], z_dev)
 
     def wait_tile(j):
         remote(raw_peer.at[j], raw_peer.at[j], x_sem.at[0], recv_sem.at[j], x_dev).wait_recv()
@@ -370,14 +373,20 @@
     def forward(i):
         j = g_mine * group + i
         wait_tile(j)
-        y_send(i, j).start()
-        z_send(i, j).start()
-
-        @pl.when(i + AHEAD < x_count)
-        def _():
+        y_send(i, j, i < RAW).start()
+        z_send(i, j, i < RAW).start()
+        if i + AHEAD < x_count:
             x_send(i + AHEAD).start()
 
-    col0 = core * tiles
+    def relay(t):
+        if t % 2 == 0:
+            j = g_z * group + t
+            wait_tile(j)
+            y_send(group + t // 2, j, t < RAW).start()
+        else:
+            j = g_y * group + t
+            wait_tile(j)
+            z_send(group + t // 2, j, t < RAW).start()
 
     def load(j):
         cols = pl.ds(pl.multiple_of((col0 + j) * LANES, LANES), LANES)
@@ -434,10 +443,7 @@
         load(load_order(n)).wait()
         return c
 
-    lax.fori_loop(0, group, wait_load, 0)
-    for i in range(AHEAD):
-        x_send(i).start()
-    lax.fori_loop(group, tiles, wait_load, 0)
+    lax.fori_loop(0, tiles, wait_load, 0)
 
     def peak_exchange(kind, value, members):
         me = seq * 2 + tp
@@ -468,10 +474,10 @@
         return finish, [out for out, _ in sends]
 
     def tile_top(j, m):
-        x = jnp.abs(raw_own[j]).reshape(-1, 4 * BLOCK, LANES)
+        x = jnp.abs(raw_own[pl.ds(4 * j, 4)]).reshape(-1, 8 * BLOCK, LANES)
         return jnp.maximum(m, jnp.max(x, axis=0))
 
-    w_top = lax.fori_loop(0, tiles, tile_top, jnp.zeros((4 * BLOCK, LANES), jnp.bfloat16))
+    w_top = lax.fori_loop(0, tiles // 4, tile_top, jnp.zeros((8 * BLOCK, LANES), jnp.bfloat16))
     w_top = jnp.full((8, LANES), jnp.max(w_top.astype(jnp.float32)), jnp.float32)
 
     def sib(s):
@@ -479,22 +485,30 @@
 
     finish_w, w_sends = peak_exchange(0, w_top, [(sib, 0), (0, 1), (sib, 1)])
 
-    remote(kv_buf.at[far], kv_buf.at[far], kv_send.at[0], kv_recv.at[far], y_dev).wait_recv()
-    kv_f.start()
-
+    for i in range(RAW):
+        x_send(i).start()
     w_inv, w_scale = scales_of(finish_w()[0:1, :])
 
     def own_copy(p):
         sl = pl.ds(col0 + 2 * p, 2)
         return remote(w_own.at[sl], w_own.at[sl], own_send.at[p], own_recv.at[p], s_dev)
 
-    def own_pair(p, c):
+    def own_pair(p):
         for t in range(2):
             quant_tile(raw_own.at[2 * p + t], w_own.at[col0 + 2 * p + t], w_inv, w_scale)
         own_copy(p).start()
-        return c
-
-    lax.fori_loop(0, OWN_FIRST, own_pair, 0)
+
+    def own_range(first, count):
+        def body(n, c):
+            own_pair(first + n)
+            return c
+
+        lax.fori_loop(0, count, body, 0)
+
+    half = group_pairs
+    own_range(g_mine * half + 1, half - 1)
+    remote(kv_buf.at[far], kv_buf.at[far], kv_send.at[0], kv_recv.at[far], y_dev).wait_recv()
+    kv_f.start()
     forward(0)
 
     for c in q_loads:
@@ -502,71 +516,108 @@
     for slot in (other, far_other):
         remote(kv_buf.at[slot], kv_buf.at[slot], kv_send.at[0], kv_recv.at[slot], s_dev).wait_recv()
 
-    rate = HEAD_SIZE ** (-0.5)
+    rate = HEAD_SIZE ** (-0.5) * 1.4426950408889634
 
     def scores_of(q, b):
         return lax.dot_general(
             q, kv_buf[b, 0], (((1,), (1,)), ((), ())), preferred_element_type=jnp.float32
         )
 
-    def attend_tile(first, h):
-        q = q_buf[h, pl.ds(first, share), :]
-        s = scores_of(q, seq)
+    def weigh(p, b):
+        return jnp.dot(p.astype(jnp.bfloat16), kv_buf[b, 1], preferred_element_type=jnp.float32)
+
+    def attend_tiles(first, h0, m):
+        qs = [q_buf[h0 + u, pl.ds(first, share), :] for u in range(2)]
         row = lax.broadcasted_iota(jnp.int32, (share, tokens), 0) + first
         col = lax.broadcasted_iota(jnp.int32, (share, tokens), 1)
-        s = jnp.where(row >= col, s, neg_large)
-        top = jnp.max(s, axis=1, keepdims=True)
-        p = jnp.exp((s - top) * rate)
-        total = jnp.sum(p, axis=1, keepdims=True)
-        acc = jnp.dot(p.astype(jnp.bfloat16), kv_buf[seq, 1], preferred_element_type=jnp.float32)
-
-        def body(b, carry):
-            top, total, acc = carry
-            s = scores_of(q, b)
-            new = jnp.maximum(top, jnp.max(s, axis=1, keepdims=True))
-            fix = jnp.exp((top - new) * rate)
-            p = jnp.exp((s - new) * rate)
-            total = total * fix + jnp.sum(p, axis=1, keepdims=True)
-            acc = acc * fix + jnp.dot(
-                p.astype(jnp.bfloat16), kv_buf[b, 1], preferred_element_type=jnp.float32
-            )
-            return new, total, acc
-
-        top, total, acc = lax.fori_loop(0, seq, body, (top, total, acc))
-        out = (acc / total).astype(jnp.bfloat16)
-        act_full[h, pl.ds(first, share), :] = out
-        return jnp.max(jnp.abs(out.astype(jnp.float32)), axis=0, keepdims=True)
+        state = []
+        for q in qs:
+            s = jnp.where(row >= col, scores_of(q, seq), neg_large)
+            top = jnp.max(s, axis=1, keepdims=True)
+            p = jnp.exp2((s - top) * rate)
+            state.append((top, jnp.sum(p, axis=1, keepdims=True), weigh(p, seq)))
+
+        def body(b, state):
+            out = []
+            for q, (top, total, acc) in zip(qs, state):
+                s = scores_of(q, b)
+                new = jnp.maximum(top, jnp.max(s, axis=1, keepdims=True))
+                fix = jnp.exp2((top - new) * rate)
+                p = jnp.exp2((s - new) * rate)
+                total = total * fix + jnp.sum(p, axis=1, keepdims=True)
+                out.append((new, total, acc * fix + weigh(p, b)))
+            return tuple(out)
+
+        for u, (top, total, acc) in enumerate(lax.fori_loop(0, seq, body, tuple(state))):
+            out = (acc / total).astype(jnp.bfloat16)
+            act_full[h0 + u, pl.ds(first, share), :] = out
+            m = jnp.maximum(m, jnp.max(jnp.abs(out.astype(jnp.float32)), axis=0, keepdims=True))
+        return m
 
     theirs = pl.multiple_of((1 - tp) * share, share)
     mine = pl.multiple_of(tp * share, share)
     a_top = jnp.zeros((1, LANES), jnp.float32)
-
-    def att_loop(first):
-        def body(h, m):
-            return jnp.maximum(m, attend_tile(first, h))
-
-        return body
-
-    a_top = lax.fori_loop(0, heads, att_loop(theirs), a_top)
     act_copy = remote(
         act_full.at[:, pl.ds(theirs, share), :], act_peer, act_sem.at[0], act_sem.at[1], x_dev
     )
+    pieces = [(theirs, h) for h in range(0, heads, 2)] + [(mine, h) for h in range(0, heads, 2)]
+
+    def att_piece(n, m):
+        late = n // (heads // 2)
+        first = pl.multiple_of((late * tp + (1 - late) * (1 - tp)) * share, share)
+        return attend_tiles(first, 2 * lax.rem(n, heads // 2), m)
+
+    a_top = lax.fori_loop(0, 1, att_piece, a_top)
+    forward(1)
+    a_top = lax.fori_loop(1, 2, att_piece, a_top)
     act_copy.start()
-    forward(1)
     forward(2)
-    a_top = lax.fori_loop(0, heads, att_loop(mine), a_top)
+    a_top = lax.fori_loop(2, 3, att_piece, a_top)
+    relay(0)
+    relay(1)
+    a_top = lax.fori_loop(3, 4, att_piece, a_top)
     a_top = jnp.full((8, LANES), jnp.max(a_top), jnp.float32)
     finish_a, a_sends = peak_exchange(1, a_top, team)
-
     forward(3)
-    third = (pairs - OWN_FIRST) // 3
-    lax.fori_loop(OWN_FIRST, OWN_FIRST + third, own_pair, 0)
+    relay(2)
+    own_range(g_d * half + half - 1, 1)
+    own_range(g_mine * half, 1)
+    own_range(g_y * half, half)
+    own_range(g_z * half, half)
     forward(4)
-    lax.fori_loop(OWN_FIRST + third, OWN_FIRST + 2 * third, own_pair, 0)
+    relay(3)
+    own_range(g_d * half, half - 1)
+    square_sum[...] = jnp.zeros_like(square_sum)
+    bm_ref[...] = jnp.zeros_like(bm_ref)
+
+    def local_pair(p):
+        late = p // (3 * group_pairs)
+        sel = lax.rem(p, 3)
+        fy = late + (1 - late) * (sel % 2)
+        fz = late + (1 - late) * (sel // 2)
+        g = lax.rem(y + fy, 2) + 2 * lax.rem(zz + fz, 2)
+        i = (1 - late) * (p // 3) + late * (p - 3 * group_pairs)
+        return g * group_pairs + i, late, sel, i
+
+    def peer_copy(lp):
+        sl = pl.ds(col0 + 2 * lp, 2)
+        return remote(w_peer.at[sl], w_peer.at[sl], peer_send.at[lp], peer_recv.at[lp], s_dev)
+
+    def take_raw(p):
+        lp = local_pair(p)[0]
+        if p == 3 * group_pairs:
+            wait_tile(2 * lp)
+            wait_tile(2 * lp + 1)
+        elif p:
+            wait_tile(2 * lp + p - 1)
+        for t in range(2):
+            quant_tile(raw_peer.at[2 * lp + t], w_peer.at[col0 + 2 * lp + t], w_inv, w_scale)
+        peer_copy(lp).start()
+
+    for p in (0, 1, 2, 3 * group_pairs):
+        take_raw(p)
     forward(5)
-    lax.fori_loop(OWN_FIRST + 2 * third, pairs, own_pair, 0)
-    for i in range(6, group):
-        forward(i)
+    relay(4)
 
     a_inv, a_scale = scales_of(finish_a()[0:1, :])
     act_copy.wait_recv()
@@ -586,95 +637,90 @@
                     payload * spacing
                 ).astype(jnp.bfloat16)
 
-    square_sum[...] = jnp.zeros_like(square_sum)
-    row_top[...] = jnp.zeros_like(row_top)
-
-    def local_pair(p):
-        late = p // (3 * group_pairs)
-        sel = lax.rem(p, 3)
-        fy = late + (1 - late) * (sel % 2)
-        fz = late + (1 - late) * (sel // 2)
-        g = lax.rem(y + fy, 2) + 2 * lax.rem(zz + fz, 2)
-        i = (1 - late) * (p // 3) + late * (p - 3 * group_pairs)
-        return g * group_pairs + i, late, sel, i
-
-    def peer_copy(lp):
-        sl = pl.ds(col0 + 2 * lp, 2)
-        return remote(w_peer.at[sl], w_peer.at[sl], peer_send.at[lp], peer_recv.at[lp], s_dev)
-
     def out_copy(n):
         cols = pl.ds(pl.multiple_of(2 * n * LANES, 2 * LANES), 2 * LANES)
         return pltpu.make_async_copy(hid_buf.at[:, cols], hid_hbm.at[:, cols], out_sem.at[n])
 
-    def project_pair(n):
+    lane = lax.broadcasted_iota(jnp.int32, (32, LANES), 1)
+    odd = lane % 2 == 1
+
+    def epilogue(n, own, peer):
         cols = pl.ds(pl.multiple_of(2 * n * LANES, 2 * LANES), 2 * LANES)
-        a = jnp.concatenate([w_own[2 * n], w_own[2 * n + 1]], axis=1)
-        b = jnp.concatenate([w_peer[2 * n], w_peer[2 * n + 1]], axis=1)
-        part_own[...] = jnp.dot(act_q[0], a, preferred_element_type=jnp.float32)
-        part_peer[...] = jnp.dot(act_q[1], b, preferred_element_type=jnp.float32)
         gain = gain_ref[:, cols]
+        mask = (lane // 2) % 8 == n % 8
+        turns = [LANES - s + 2 * s * ((2 * n // s) % 2) for s in (2, 4, 8)]
         for lo in range(0, share, 32):
-            p0 = part_own[lo : lo + 32, :].astype(jnp.bfloat16).astype(jnp.float32)
-            p1 = part_peer[lo : lo + 32, :].astype(jnp.bfloat16).astype(jnp.float32)
+            p0 = own[lo : lo + 32, :].astype(jnp.bfloat16).astype(jnp.float32)
+            p1 = peer[lo : lo + 32, :].astype(jnp.bfloat16).astype(jnp.float32)
             h = res_buf[lo : lo + 32, cols].astype(jnp.float32) + (p0 + p1)
             hid_buf[lo : lo + 32, cols] = h
             s = jnp.abs(h * gain)
             h = h * h
             square_sum[lo : lo + 32, :] += h[:, :LANES] + h[:, LANES:]
-            row_top[lo : lo + 32, :] = jnp.maximum(
-                row_top[lo : lo + 32, :], jnp.maximum(s[:, :LANES], s[:, LANES:])
-            )
-        out_copy(n).start()
+            m0, m1 = s[:, :LANES], s[:, LANES:]
+            m0 = jnp.maximum(m0, pltpu.roll(m0, LANES - 1, 1))
+            m1 = jnp.maximum(m1, pltpu.roll(m1, 1, 1))
+            m = jnp.where(odd, m1, m0)
+            for turn in turns:
+                m = jnp.maximum(m, pltpu.roll(m, turn, 1))
+            bm_ref[n // 8, lo : lo + 32, :] = jnp.where(mask, m, bm_ref[n // 8, lo : lo + 32, :])
+
+    def product(k, w, n):
+        w = jnp.concatenate([w[2 * n], w[2 * n + 1]], axis=1)
+        return jnp.dot(act_q[k], w, preferred_element_type=jnp.float32)
+
+    def project(pair_ids):
+        parts = [(product(0, w_own, n), product(1, w_peer, n)) for n in pair_ids]
+        for n, (own, peer) in zip(pair_ids, parts):
+            epilogue(n, own, peer)
+        for n in pair_ids:
+            out_copy(n).start()
 
     other0 = (1 - core) * tiles
 
-    def sibling_pair(lp):
+    def take(p):
+        lp, late, sel, i = local_pair(p)
+
+        @pl.when((1 - late) * sel * (i // (group_pairs - 1)) + late > 0)
+        def _():
+            wait_tile(2 * lp)
+            wait_tile(2 * lp + 1)
+
+        @pl.when((1 - late) * sel * (1 - i // (group_pairs - 1)) > 0)
+        def _():
+            wait_tile(2 * lp + sel - 1)
+
+        peer_copy(lp).start()
+
+    res_load.wait()
+    forward(6)
+
+    def step(p, c):
+        @pl.when(p == 1)
+        def _():
+            relay(5)
+
+        @pl.when(p == 2)
+        def _():
+            forward(7)
+
+        @pl.when((p > 1) * (p < pairs - 1) * (p + 1 != 3 * group_pairs))
+        def _():
+            take(p + 1)
+
+        lp = local_pair(p)[0]
         sl = pl.ds(other0 + 2 * lp, 2)
         remote(w_own.at[sl], w_own.at[sl], own_send.at[0], own_recv.at[lp], s_dev).wait_recv()
         remote(w_peer.at[sl], w_peer.at[sl], peer_send.at[0], peer_recv.at[lp], s_dev).wait_recv()
-        project_pair(other0 // 2 + lp)
-
-    res_load.wait()
-
-    def step(p, c):
-        lp, late, sel, i = local_pair(p)
-
-        @pl.when(late + sel > 0)
-        def _():
-            wait_tile(2 * lp)
-            wait_tile(2 * lp + 1)
-
-        @pl.when((1 - late) * sel * (sel % 2) * (2 * i // (relay_x + relay_y)) > 0)
-        def _():
-            for t in range(2):
-                n = 2 * i + t - relay_x - relay_y
-                z_send(group + n, 2 * lp + t).start()
-
-        for lo in range(relay_x // 2, (relay_x + relay_y) // 2):
-            @pl.when((1 - late) * (sel // 2) * (1 - (i - lo) * (i - lo)) > 0)
-            def _():
-                for t in range(2):
-                    n = 2 * (lo - relay_x // 2) + t
-                    y_send(group + n, 2 * lp + t).start()
-
-        for t in range(2):
-            quant_tile(raw_peer.at[2 * lp + t], w_peer.at[col0 + 2 * lp + t], w_inv, w_scale)
-        peer_copy(lp).start()
-        project_pair(col0 // 2 + lp)
-
-        @pl.when(p > 0)
-        def _():
-            sibling_pair(local_pair(p - 1)[0])
-
+        project([col0 // 2 + lp, other0 // 2 + lp])
         return c
 
     lax.fori_loop(0, pairs, step, 0)
-    sibling_pair(local_pair(pairs - 1)[0])
 
     mean_square = jnp.sum(square_sum[...], axis=1, keepdims=True) / features
     rstd = lax.rsqrt(mean_square + 1e-05)
     rstd_ref[...] = jnp.broadcast_to(rstd, rstd_ref.shape)
-    n_top = jnp.max(jnp.max(row_top[...], axis=1, keepdims=True) * rstd)
+    n_top = jnp.max(jnp.max(bm_ref[...], axis=0) * rstd)
     finish_n, n_sends = peak_exchange(2, jnp.full((8, LANES), n_top, jnp.float32), team)
 
     kv_y.wait_send()
@@ -693,18 +739,18 @@
 
     lax.fori_loop(0, pairs, drain, 0)
 
-    def drain_links(i, c):
+    def drain_x(i, c):
         remote(raw_own.at[0], raw_peer.at[0], x_sem.at[i], recv_sem.at[0], x_dev).wait_send()
+        return c
+
+    lax.fori_loop(0, x_count, drain_x, 0)
+
+    def drain_yz(i, c):
         y_send(i, 0).wait_send()
-        return c
-
-    lax.fori_loop(0, x_count, drain_links, 0)
-
-    def drain_z(i, c):
         z_send(i, 0).wait_send()
         return c
 
-    lax.fori_loop(0, z_count, drain_z, 0)
+    lax.fori_loop(0, y_count, drain_yz, 0)
     top_ref[...] = finish_n()
     for c in n_sends:
         c.wait_send()
@@ -725,11 +771,12 @@
     return pl.pallas_call(
         functools.partial(fused_kernel, features=d),
         in_specs=[any_spec] * 5 + [vmem],
-        out_specs=[any_spec, vmem, vmem],
+        out_specs=[any_spec, vmem, vmem, vmem],
         out_shape=[
             jax.ShapeDtypeStruct((share, d), f32),
             jax.ShapeDtypeStruct((share, LANES), f32),
             jax.ShapeDtypeStruct((8, LANES), f32),
+            jax.ShapeDtypeStruct((d // (BLOCK * LANES), share, LANES), f32),
         ],
         scratch_shapes=[
             pltpu.VMEM((heads, tokens, HEAD_SIZE), bf16),
@@ -744,16 +791,13 @@
             pltpu.VMEM((heads, share, HEAD_SIZE), bf16),
             pltpu.VMEM((2, share, n_feat), bf16),
             pltpu.VMEM((share, LANES), f32),
-            pltpu.VMEM((share, LANES), f32),
             pltpu.VMEM((3, 8, 8, LANES), f32),
-            pltpu.VMEM((share, 2 * LANES), f32),
-            pltpu.VMEM((share, 2 * LANES), f32),
             dma((3 + heads,)),
             dma((tiles,)),
             dma((tiles,)),
             dma((group + group // 4,)),
-            dma((group + group // 4,)),
-            dma((2 * group - 2 * (group // 4),)),
+            dma((group + 3 * group // 8,)),
+            dma((group + 3 * group // 8,)),
             dma((3,)),
             dma((4,)),
             dma((3, 7)),
@@ -772,48 +816,64 @@
     )(queries, keys, values, out_weight, residual, gain)
 
 
-def final_fast_kernel(top_ref, hid_ref, rstd_ref, gain_ref, new_ref, out_ref, narrow, wide):
-    rows, cols = hid_ref.shape
+def two_parts(x):
+    high = x.astype(jnp.bfloat16)
+    low = (x - high.astype(jnp.float32)).astype(jnp.bfloat16)
+    return jnp.concatenate([high, low], axis=1)
+
+
+def final_fast_kernel(top_ref, hid_ref, rstd_ref, bm_ref, gain_ref, wide_ref, new_ref, out_ref):
+    rows = hid_ref.shape[0]
+    groups = bm_ref.shape[0]
     inv, tensor_scale = scales_of(top_ref[0:1, :])
-    spread = spread_matrix()
     rstd = rstd_ref[...]
-    pieces = cols // LANES
-    for i in range(pieces):
-        sl = slice(i * LANES, (i + 1) * LANES)
-        h = hid_ref[:, sl]
-        new_ref[:, sl] = h.astype(jnp.bfloat16)
-        m = lane_block_max(jnp.abs(h * rstd * gain_ref[:, sl]))
-        narrow[i * rows : (i + 1) * rows, :] = jnp.maximum(m * inv, scale_floor).astype(jnp.bfloat16)
-    wide[...] = jnp.dot(narrow[...], spread, preferred_element_type=jnp.float32)
-    for i in range(pieces):
-        sl = slice(i * LANES, (i + 1) * LANES)
-        x = hid_ref[:, sl] * rstd * gain_ref[:, sl]
-        spacing = wide[i * rows : (i + 1) * rows, :] * tensor_scale
-        payload = soft_grid(x * pl.reciprocal(spacing)).astype(jnp.bfloat16).astype(jnp.float32)
-        out_ref[:, sl] = (payload * spacing).astype(jnp.bfloat16)
-
-
-def final_fast(top, hidden, rstd, gain):
+    rates, spacings = [], []
+    for g in range(groups):
+        scale = jnp.maximum(bm_ref[g] * rstd * inv, scale_floor).astype(jnp.bfloat16)
+        spacing = scale.astype(jnp.float32) * tensor_scale
+        rates.append(two_parts(rstd / spacing))
+        spacings.append(two_parts(spacing))
+    rates = jnp.concatenate(rates, axis=0)
+    spacings = jnp.concatenate(spacings, axis=0)
+    width = 2 * LANES
+    for v in range(BLOCK // 2):
+        wide = wide_ref[:, v * width : (v + 1) * width]
+        rate = jnp.dot(rates, wide, preferred_element_type=jnp.float32)
+        spacing = jnp.dot(spacings, wide, preferred_element_type=jnp.float32)
+        for g in range(groups):
+            lo = (g * BLOCK // 2 + v) * width
+            h = hid_ref[:, lo : lo + width]
+            new_ref[:, lo : lo + width] = h.astype(jnp.bfloat16)
+            u = (h * gain_ref[:, lo : lo + width]) * rate[g * rows : (g + 1) * rows]
+            payload = soft_grid(u).astype(jnp.bfloat16).astype(jnp.float32)
+            out_ref[:, lo : lo + width] = (payload * spacing[g * rows : (g + 1) * rows]).astype(
+                jnp.bfloat16
+            )
+
+
+def final_fast(top, hidden, rstd, block_max, gain):
     tokens, d = hidden.shape
-    width, rows = 2048, 64
-    column = pl.BlockSpec((rows, width), lambda i, j: (i, j))
+    groups = block_max.shape[0]
+    rows = 64
+    src = np.arange(2 * LANES)[:, None] % LANES
+    dst = np.arange(BLOCK * LANES)[None, :]
+    wide = jnp.asarray(src == dst % LANES // BLOCK * BLOCK + dst // LANES, jnp.bfloat16)
+    line = pl.BlockSpec((rows, d), lambda i: (i, 0))
     return pl.pallas_call(
         final_fast_kernel,
-        grid=(tokens // rows, d // width),
+        grid=(tokens // rows,),
         in_specs=[
-            pl.BlockSpec((8, LANES), lambda i, j: (0, 0)),
-            column,
-            pl.BlockSpec((rows, LANES), lambda i, j: (i, 0)),
-            pl.BlockSpec((1, width), lambda i, j: (0, j)),
+            pl.BlockSpec((8, LANES), lambda i: (0, 0)),
+            line,
+            pl.BlockSpec((rows, LANES), lambda i: (i, 0)),
+            pl.BlockSpec((groups, rows, LANES), lambda i: (0, i, 0)),
+            pl.BlockSpec((1, d), lambda i: (0, 0)),
+            pl.BlockSpec((2 * LANES, BLOCK * LANES), lambda i: (0, 0)),
         ],
-        out_specs=[column, column],
+        out_specs=[line, line],
         out_shape=[jax.ShapeDtypeStruct((tokens, d), jnp.bfloat16)] * 2,
-        scratch_shapes=[
-            pltpu.VMEM((rows * width // LANES, LANES), jnp.bfloat16),
-            pltpu.VMEM((rows * width // LANES, LANES), jnp.float32),
-        ],
         name="final_fast",
-    )(top, hidden, rstd, gain)
+    )(top, hidden, rstd, block_max, gain, wide)
 
 
 def fits_fused(queries, keys, out_weight, residual):
@@ -835,8 +895,8 @@
     if not fits_fused(queries, keys, out_weight, residual):
         return general(queries, keys, values, out_weight, residual, norm_gain)
     gain = norm_gain.astype(jnp.float32).reshape(1, -1)
-    hidden, rstd, top = fused(queries, keys, values, out_weight, residual, gain)
-    return tuple(final_fast(top, hidden, rstd, gain))
+    hidden, rstd, top, block_max = fused(queries, keys, values, out_weight, residual, gain)
+    return tuple(final_fast(top, hidden, rstd, block_max, gain))
 
 
 def solution(mesh):

time: 101 us -> 78.3 us (0.78)
  Pallas kernels: 98.8 us -> 76 us
    pallas_call x1, Pallas kernels: 78.5 us -> 64.8 us  [fused(): pl.pallas_call(functools.partial(fused_kernel, features=d), in_specs=[any...]
    pallas_call x1, Pallas kernels: 20.3 us -> 11.1 us  [final_fast(): pl.pallas_call(final_fast_kernel, grid=(tokens // rows,), in_specs=[pl.Bl...]
where the time goes in v2:
time: 78.3 us; the launch traced here: 77.9 us
  Pallas kernels  76 us (97%)
  other arithmetic  1.33 us (2%)
    pallas_call x1, Pallas kernels, fused(): pl.pallas_call(functools.partial(fused_kernel, features=d), in_specs=[any...  64.8 us
    pallas_call x1, Pallas kernels, final_fast(): pl.pallas_call(final_fast_kernel, grid=(tokens // rows,), in_specs=[pl.Bl...  11.1 us

profile of v2, /device:TPU:0, one launch (start us, length us, event | category | flops | bytes accessed | tf_op | source)
XLA Modules:
  0.0 77.9 jit_solution(2900590265483456713)
XLA Ops:
  0.6 1.3 %reshape.11 = f32[8192]{0:T(1024)} convert(bf16[8192]{0:T(1024)(128)(2,1)} %param.12) | non-fusion elementwise | flops 8192 | bytes 49152 | tf_op jit(solution)/shard_map/reshape | solution.py:897
  2.0 64.8 %fused.1 = (f32[256,8192]{1,0:T(8,128)}, f32[256,128]{1,0:T(8,128)}, f32[8,128]{1,0:T(8,128)}, f32[4,256,128]{2,1,0:T(8,128)}) custom-call(bf16[512,512]{1,0:T(8,128)(2,1)} %q_hbm.1, bf16[512,128]{1,0:T(8,128)(2,1)} %k_hbm.1, bf16[512,128]{1,0:T(8,128)(2,1)} %v_hbm.1, bf16[512,8192]{1,0:T(8,128)(2,1)} %w_hbm.1, bf16[256,8192]{1,0:T(8,128)(2,1)} %res_hbm.1, ...), custom_call_target="tpu_custom_call" | custom-call | tf_op jit(solution)/shard_map/fused/pallas_call | solution.py:771
  66.8 11.1 %final_fast.1 = (bf16[256,8192]{1,0:T(8,128)(2,1)}, bf16[256,8192]{1,0:T(8,128)(2,1)}) custom-call(f32[8,128]{1,0:T(8,128)} %get-tuple-element.6.top_ref, f32[256,8192]{1,0:T(8,128)} %get-tuple-element.7.hid_ref, f32[256,128]{1,0:T(8,128)} %get-tuple-element.8.rstd_ref, f32[4,256,128]{2,1,0:T(8,128)} %get-tuple-element.9.bm_ref, f32[1,8192]{1,0:T(1,128)} %bitcast.2, ...), custom_call_target="tpu_custom_call" | custom-call | tf_op jit(solution)/shard_map/final_fast/pallas_call | solution.py:862

commit v3 on v2

--- a/solution.py
+++ b/solution.py
@@ -300,23 +300,46 @@
     return 1.0 / (6.0 * tensor_scale), tensor_scale
 
 
-def lane_block_max(m):
-    for s in (1, 2, 4, 8):
-        m = jnp.maximum(m, pltpu.roll(m, s, 1))
-    return m
+def block_maxima(parts):
+    lane = lax.broadcasted_iota(jnp.int32, parts[0].shape, 1)
+    s = 1
+    while s < BLOCK:
+        if len(parts) == 1:
+            m = parts[0]
+            turned = jnp.where(lane // s % 2 == 1, pltpu.roll(m, s, 1), pltpu.roll(m, LANES - s, 1))
+            parts = [jnp.maximum(m, turned)]
+        else:
+            parts = [
+                jnp.where(
+                    lane // s % 2 == 1,
+                    jnp.maximum(b, pltpu.roll(b, s, 1)),
+                    jnp.maximum(a, pltpu.roll(a, LANES - s, 1)),
+                )
+                for a, b in zip(parts[::2], parts[1::2])
+            ]
+        s *= 2
+    return parts[0]
+
+
+def two_parts(x):
+    high = x.astype(jnp.bfloat16)
+    low = (x - high.astype(jnp.float32)).astype(jnp.bfloat16)
+    return jnp.concatenate([high, low], axis=1)
 
 
 def spread_matrix():
-    src = lax.broadcasted_iota(jnp.int32, (LANES, LANES), 0)
-    dst = lax.broadcasted_iota(jnp.int32, (LANES, LANES), 1)
-    return jnp.where(src == (dst // BLOCK) * BLOCK + BLOCK - 1, 1.0, 0.0).astype(jnp.bfloat16)
+    src = np.arange(2 * LANES)[:, None] % LANES
+    dst = np.arange(BLOCK * LANES)[None, :]
+    wide = src == dst % LANES // BLOCK * BLOCK + dst // LANES
+    return jnp.asarray(wide, jnp.bfloat16)
 
 
 def fused_kernel(
-    q_hbm, k_hbm, v_hbm, w_hbm, res_hbm, gain_ref,
+    q_hbm, k_hbm, v_hbm, w_hbm, res_hbm, gain_ref, wide_ref,
     hid_hbm, rstd_ref, top_ref, bm_ref,
     q_buf, kv_buf, raw_own, raw_peer, w_own, w_peer, res_buf, hid_buf,
     act_full, act_peer, act_q, square_sum, peaks,
+    score_a, score_b, top_a, top_b, weights, total, acc, parts_a, parts_b, gain_f,
     local_sem, load_sem, recv_sem, x_sem, y_sem, z_sem,
     kv_send, kv_recv, peak_send, peak_recv, act_sem,
     own_send, own_recv, peer_send, peer_recv, out_sem,
@@ -443,7 +466,9 @@
         load(load_order(n)).wait()
         return c
 
-    lax.fori_loop(0, tiles, wait_load, 0)
+    wait_load(0, 0)
+    x_send(0).start()
+    lax.fori_loop(1, tiles, wait_load, 0)
 
     def peak_exchange(kind, value, members):
         me = seq * 2 + tp
@@ -474,18 +499,24 @@
         return finish, [out for out, _ in sends]
 
     def tile_top(j, m):
-        x = jnp.abs(raw_own[pl.ds(4 * j, 4)]).reshape(-1, 8 * BLOCK, LANES)
-        return jnp.maximum(m, jnp.max(x, axis=0))
-
-    w_top = lax.fori_loop(0, tiles // 4, tile_top, jnp.zeros((8 * BLOCK, LANES), jnp.bfloat16))
-    w_top = jnp.full((8, LANES), jnp.max(w_top.astype(jnp.float32)), jnp.float32)
+        high, low = m
+        for t in range(4):
+            x = raw_own[4 * j + t].reshape(-1, 8 * BLOCK, LANES)
+            high = jnp.maximum(high, jnp.max(x, axis=0))
+            low = jnp.minimum(low, jnp.min(x, axis=0))
+        return high, low
+
+    zero = jnp.zeros((8 * BLOCK, LANES), jnp.bfloat16)
+    w_high, w_low = lax.fori_loop(0, tiles // 4, tile_top, (zero, zero))
+    w_top = jnp.maximum(w_high.astype(jnp.float32), -w_low.astype(jnp.float32))
+    w_top = jnp.full((8, LANES), jnp.max(w_top), jnp.float32)
 
     def sib(s):
         return (s // 2) * 2 + 1 - s % 2
 
     finish_w, w_sends = peak_exchange(0, w_top, [(sib, 0), (0, 1), (sib, 1)])
 
-    for i in range(RAW):
+    for i in range(1, RAW):
         x_send(i).start()
     w_inv, w_scale = scales_of(finish_w()[0:1, :])
 
@@ -506,10 +537,11 @@
         lax.fori_loop(0, count, body, 0)
 
     half = group_pairs
-    own_range(g_mine * half + 1, half - 1)
+    own_range(g_mine * half + 1, 1)
+    forward(0)
+    own_range(g_mine * half + 2, half - 2)
     remote(kv_buf.at[far], kv_buf.at[far], kv_send.at[0], kv_recv.at[far], y_dev).wait_recv()
     kv_f.start()
-    forward(0)
 
     for c in q_loads:
         c.wait()
@@ -518,77 +550,91 @@
 
     rate = HEAD_SIZE ** (-0.5) * 1.4426950408889634
 
-    def scores_of(q, b):
-        return lax.dot_general(
-            q, kv_buf[b, 0], (((1,), (1,)), ((), ())), preferred_element_type=jnp.float32
-        )
-
-    def weigh(p, b):
-        return jnp.dot(p.astype(jnp.bfloat16), kv_buf[b, 1], preferred_element_type=jnp.float32)
-
-    def attend_tiles(first, h0, m):
-        qs = [q_buf[h0 + u, pl.ds(first, share), :] for u in range(2)]
-        row = lax.broadcasted_iota(jnp.int32, (share, tokens), 0) + first
-        col = lax.broadcasted_iota(jnp.int32, (share, tokens), 1)
-        state = []
-        for q in qs:
-            s = jnp.where(row >= col, scores_of(q, seq), neg_large)
-            top = jnp.max(s, axis=1, keepdims=True)
-            p = jnp.exp2((s - top) * rate)
-            state.append((top, jnp.sum(p, axis=1, keepdims=True), weigh(p, seq)))
-
-        def body(b, state):
-            out = []
-            for q, (top, total, acc) in zip(qs, state):
-                s = scores_of(q, b)
-                new = jnp.maximum(top, jnp.max(s, axis=1, keepdims=True))
-                fix = jnp.exp2((top - new) * rate)
-                p = jnp.exp2((s - new) * rate)
-                total = total * fix + jnp.sum(p, axis=1, keepdims=True)
-                out.append((new, total, acc * fix + weigh(p, b)))
-            return tuple(out)
-
-        for u, (top, total, acc) in enumerate(lax.fori_loop(0, seq, body, tuple(state))):
-            out = (acc / total).astype(jnp.bfloat16)
-            act_full[h0 + u, pl.ds(first, share), :] = out
-            m = jnp.maximum(m, jnp.max(jnp.abs(out.astype(jnp.float32)), axis=0, keepdims=True))
+    def lanes_of(x):
+        return [x[:, lo : lo + LANES] for lo in range(0, tokens, LANES)]
+
+    def scores(first, h0, b, diagonal, out, top):
+        for u in range(2):
+            q = q_buf[h0 + u, pl.ds(first, share), :]
+            s = lax.dot_general(
+                q, kv_buf[b, 0], (((1,), (1,)), ((), ())), preferred_element_type=jnp.float32
+            )
+            if diagonal:
+                row = lax.broadcasted_iota(jnp.int32, (share, tokens), 0) + first
+                col = lax.broadcasted_iota(jnp.int32, (share, tokens), 1)
+                s = jnp.where(row >= col, s, neg_large)
+            rows = slice(u * share, (u + 1) * share)
+            out[b, rows, :] = s
+            top[rows, :] = functools.reduce(jnp.maximum, lanes_of(s), top[rows, :])
+
+    def weigh(b, source, top):
+        for lo in range(0, tokens, 32):
+            rows = slice(lo, lo + 32)
+            shift = top[rows, :]
+            p = [jnp.exp2(x * rate - shift) for x in lanes_of(source[b, rows, :])]
+            total[rows, :] += functools.reduce(jnp.add, p)
+            weights[rows, :] = jnp.concatenate(p, axis=1).astype(jnp.bfloat16)
+        acc[...] += jnp.dot(weights[...], kv_buf[b, 1], preferred_element_type=jnp.float32)
+
+    def attend(now, later):
+        def block(b, diagonal):
+            if later:
+                scores(later[0], later[1], b, diagonal, later[2], later[3])
+            if now:
+                weigh(b, now[2], now[3])
+
+        def body(b, c):
+            block(b, False)
+            return c
+
+        if later:
+            later[3][...] = jnp.full_like(later[3], neg_large)
+        if now:
+            total[...] = jnp.zeros_like(total)
+            acc[...] = jnp.zeros_like(acc)
+        lax.fori_loop(0, seq, body, 0)
+        block(seq, True)
+        if later:
+            top = jnp.max(later[3][...], axis=1, keepdims=True) * rate
+            later[3][...] = jnp.broadcast_to(top, later[3].shape)
+        m = jnp.zeros((1, LANES), jnp.float32)
+        if now:
+            out = (acc[...] / jnp.sum(total[...], axis=1, keepdims=True)).astype(jnp.bfloat16)
+            for u in range(2):
+                act_full[now[1] + u, pl.ds(now[0], share), :] = out[u * share : (u + 1) * share]
+            m = jnp.max(jnp.abs(out.astype(jnp.float32)), axis=0, keepdims=True)
         return m
 
     theirs = pl.multiple_of((1 - tp) * share, share)
     mine = pl.multiple_of(tp * share, share)
-    a_top = jnp.zeros((1, LANES), jnp.float32)
     act_copy = remote(
         act_full.at[:, pl.ds(theirs, share), :], act_peer, act_sem.at[0], act_sem.at[1], x_dev
     )
-    pieces = [(theirs, h) for h in range(0, heads, 2)] + [(mine, h) for h in range(0, heads, 2)]
-
-    def att_piece(n, m):
-        late = n // (heads // 2)
-        first = pl.multiple_of((late * tp + (1 - late) * (1 - tp)) * share, share)
-        return attend_tiles(first, 2 * lax.rem(n, heads // 2), m)
-
-    a_top = lax.fori_loop(0, 1, att_piece, a_top)
+    jobs = [(theirs, 0), (theirs, 2), (mine, 0), (mine, 2)]
+    jobs = [j + ((score_a, top_a) if n % 2 == 0 else (score_b, top_b)) for n, j in enumerate(jobs)]
     forward(1)
-    a_top = lax.fori_loop(1, 2, att_piece, a_top)
-    act_copy.start()
+    attend(None, jobs[0])
     forward(2)
-    a_top = lax.fori_loop(2, 3, att_piece, a_top)
+    a_top = attend(jobs[0], jobs[1])
     relay(0)
     relay(1)
-    a_top = lax.fori_loop(3, 4, att_piece, a_top)
+    a_top = jnp.maximum(a_top, attend(jobs[1], jobs[2]))
+    act_copy.start()
+    a_top = jnp.maximum(a_top, attend(jobs[2], jobs[3]))
+    a_top = jnp.maximum(a_top, attend(jobs[3], None))
     a_top = jnp.full((8, LANES), jnp.max(a_top), jnp.float32)
     finish_a, a_sends = peak_exchange(1, a_top, team)
     forward(3)
-    relay(2)
     own_range(g_d * half + half - 1, 1)
     own_range(g_mine * half, 1)
+    forward(4)
     own_range(g_y * half, half)
+    relay(2)
     own_range(g_z * half, half)
-    forward(4)
     relay(3)
+    forward(5)
     own_range(g_d * half, half - 1)
     square_sum[...] = jnp.zeros_like(square_sum)
-    bm_ref[...] = jnp.zeros_like(bm_ref)
 
     def local_pair(p):
         late = p // (3 * group_pairs)
@@ -614,67 +660,97 @@
             quant_tile(raw_peer.at[2 * lp + t], w_peer.at[col0 + 2 * lp + t], w_inv, w_scale)
         peer_copy(lp).start()
 
-    for p in (0, 1, 2, 3 * group_pairs):
+    for p in (0, 1):
         take_raw(p)
-    forward(5)
+    forward(6)
     relay(4)
+    for p in (2, 3 * group_pairs):
+        take_raw(p)
 
     a_inv, a_scale = scales_of(finish_a()[0:1, :])
     act_copy.wait_recv()
-    spread = spread_matrix()
-    for k in range(2):
-        for h in range(heads):
-            for lo in range(0, share, 64):
-                if k == 0:
-                    x = act_full[h, pl.ds(mine + lo, 64), :].astype(jnp.float32)
-                else:
-                    x = act_peer[h, lo : lo + 64, :].astype(jnp.float32)
-                m = lane_block_max(jnp.abs(x))
-                narrow = jnp.maximum(m * a_inv, scale_floor).astype(jnp.bfloat16)
-                spacing = jnp.dot(narrow, spread, preferred_element_type=jnp.float32) * a_scale
-                payload = soft_grid(x * (1.0 / spacing)).astype(jnp.bfloat16).astype(jnp.float32)
-                act_q[k, lo : lo + 64, h * HEAD_SIZE : (h + 1) * HEAD_SIZE] = (
-                    payload * spacing
-                ).astype(jnp.bfloat16)
+    def act_tile(t, lo, n):
+        if t < heads:
+            return act_full[t, pl.ds(mine + lo, n), :].astype(jnp.float32)
+        return act_peer[t - heads, lo : lo + n, :].astype(jnp.float32)
+
+    rates, spacings = [], []
+    for lo in range(0, share, 16):
+        m = block_maxima([jnp.abs(act_tile(t, lo, 16)) for t in range(2 * heads)])
+        scale = jnp.maximum(m * a_inv, scale_floor).astype(jnp.bfloat16)
+        spacing = scale.astype(jnp.float32) * a_scale
+        rates.append(two_parts(1.0 / spacing))
+        spacings.append(two_parts(spacing))
+    rates = jnp.concatenate(rates, axis=0)
+    spacings = jnp.concatenate(spacings, axis=0)
+    for t in range(0, 2 * heads, 2):
+        cols = wide_ref[:, t * LANES : (t + 2) * LANES]
+        rate = jnp.dot(rates, cols, preferred_element_type=jnp.float32)
+        spacing = jnp.dot(spacings, cols, preferred_element_type=jnp.float32)
+        for lo in range(0, share, 32):
+            x = jnp.concatenate([act_tile(t, lo, 32), act_tile(t + 1, lo, 32)], axis=1)
+            payload = soft_grid(x * rate[lo : lo + 32]).astype(jnp.bfloat16).astype(jnp.float32)
+            first = t % heads * LANES
+            act_q[t // heads, lo : lo + 32, first : first + 2 * LANES] = (
+                payload * spacing[lo : lo + 32]
+            ).astype(jnp.bfloat16)
 
     def out_copy(n):
         cols = pl.ds(pl.multiple_of(2 * n * LANES, 2 * LANES), 2 * LANES)
         return pltpu.make_async_copy(hid_buf.at[:, cols], hid_hbm.at[:, cols], out_sem.at[n])
 
     lane = lax.broadcasted_iota(jnp.int32, (32, LANES), 1)
-    odd = lane % 2 == 1
-
-    def epilogue(n, own, peer):
-        cols = pl.ds(pl.multiple_of(2 * n * LANES, 2 * LANES), 2 * LANES)
-        gain = gain_ref[:, cols]
-        mask = (lane // 2) % 8 == n % 8
-        turns = [LANES - s + 2 * s * ((2 * n // s) % 2) for s in (2, 4, 8)]
+
+    def finish(p, parts):
+        lp, _, _, i = local_pair(p)
+        pair_ids = (lp, lp + pairs)
+        cols = [pl.ds(pl.multiple_of(2 * n * LANES, 2 * LANES), 2 * LANES) for n in pair_ids]
+        gains = [
+            jnp.concatenate([gain_f[pl.ds(2 * n, 1), :], gain_f[pl.ds(2 * n + 1, 1), :]], axis=1)
+            for n in pair_ids
+        ]
+        mask = lane // 4 % 4 == i
+        turns = [LANES - s + 2 * s * ((4 * i // s) % 2) for s in (4, 8)]
         for lo in range(0, share, 32):
-            p0 = own[lo : lo + 32, :].astype(jnp.bfloat16).astype(jnp.float32)
-            p1 = peer[lo : lo + 32, :].astype(jnp.bfloat16).astype(jnp.float32)
-            h = res_buf[lo : lo + 32, cols].astype(jnp.float32) + (p0 + p1)
-            hid_buf[lo : lo + 32, cols] = h
-            s = jnp.abs(h * gain)
-            h = h * h
-            square_sum[lo : lo + 32, :] += h[:, :LANES] + h[:, LANES:]
-            m0, m1 = s[:, :LANES], s[:, LANES:]
-            m0 = jnp.maximum(m0, pltpu.roll(m0, LANES - 1, 1))
-            m1 = jnp.maximum(m1, pltpu.roll(m1, 1, 1))
-            m = jnp.where(odd, m1, m0)
+            rows = slice(lo, lo + 32)
+            maxima = []
+            squares = square_sum[rows, :]
+            for u in range(2):
+                p0 = parts[2 * u, rows, :].astype(jnp.bfloat16).astype(jnp.float32)
+                p1 = parts[2 * u + 1, rows, :].astype(jnp.bfloat16).astype(jnp.float32)
+                h = res_buf[rows, cols[u]].astype(jnp.float32) + (p0 + p1)
+                hid_buf[rows, cols[u]] = h
+                s = jnp.abs(h * gains[u])
+                h = h * h
+                squares = squares + (h[:, :LANES] + h[:, LANES:])
+                maxima += [s[:, :LANES], s[:, LANES:]]
+            square_sum[rows, :] = squares
+            for s in (1, 2):
+                maxima = [
+                    jnp.where(
+                        lane // s % 2 == 1,
+                        jnp.maximum(b, pltpu.roll(b, s, 1)),
+                        jnp.maximum(a, pltpu.roll(a, LANES - s, 1)),
+                    )
+                    for a, b in zip(maxima[::2], maxima[1::2])
+                ]
+            m = maxima[0]
             for turn in turns:
                 m = jnp.maximum(m, pltpu.roll(m, turn, 1))
-            bm_ref[n // 8, lo : lo + 32, :] = jnp.where(mask, m, bm_ref[n // 8, lo : lo + 32, :])
+            g = lp // group_pairs
+            bm_ref[g, rows, :] = jnp.where(mask, m, bm_ref[g, rows, :])
+        for n in pair_ids:
+            out_copy(n).start()
 
     def product(k, w, n):
         w = jnp.concatenate([w[2 * n], w[2 * n + 1]], axis=1)
         return jnp.dot(act_q[k], w, preferred_element_type=jnp.float32)
 
-    def project(pair_ids):
-        parts = [(product(0, w_own, n), product(1, w_peer, n)) for n in pair_ids]
-        for n, (own, peer) in zip(pair_ids, parts):
-            epilogue(n, own, peer)
-        for n in pair_ids:
-            out_copy(n).start()
+    def multiply(p, parts):
+        lp = local_pair(p)[0]
+        for u, n in enumerate((lp, lp + pairs)):
+            parts[2 * u] = product(0, w_own, n)
+            parts[2 * u + 1] = product(1, w_peer, n)
 
     other0 = (1 - core) * tiles
 
@@ -693,17 +769,11 @@
         peer_copy(lp).start()
 
     res_load.wait()
-    forward(6)
-
-    def step(p, c):
-        @pl.when(p == 1)
-        def _():
-            relay(5)
-
-        @pl.when(p == 2)
-        def _():
-            forward(7)
-
+    gain_f[...] = gain_ref[...].astype(jnp.float32)
+    forward(7)
+    relay(5)
+
+    def step(p, parts, before):
         @pl.when((p > 1) * (p < pairs - 1) * (p + 1 != 3 * group_pairs))
         def _():
             take(p + 1)
@@ -712,10 +782,23 @@
         sl = pl.ds(other0 + 2 * lp, 2)
         remote(w_own.at[sl], w_own.at[sl], own_send.at[0], own_recv.at[lp], s_dev).wait_recv()
         remote(w_peer.at[sl], w_peer.at[sl], peer_send.at[0], peer_recv.at[lp], s_dev).wait_recv()
-        project([col0 // 2 + lp, other0 // 2 + lp])
+        multiply(p, parts)
+        if before is not None:
+            finish(p - 1, before)
+
+    step(0, parts_a, None)
+
+    def two_steps(r, c):
+        p = 2 * r + 1
+
+        step(p, parts_b, parts_a)
+
+        step(p + 1, parts_a, parts_b)
         return c
 
-    lax.fori_loop(0, pairs, step, 0)
+    lax.fori_loop(0, pairs // 2 - 1, two_steps, 0)
+    step(pairs - 1, parts_b, parts_a)
+    finish(pairs - 1, parts_b)
 
     mean_square = jnp.sum(square_sum[...], axis=1, keepdims=True) / features
     rstd = lax.rsqrt(mean_square + 1e-05)
@@ -756,7 +839,7 @@
         c.wait_send()
 
 
-def fused(queries, keys, values, out_weight, residual, gain):
+def fused(queries, keys, values, out_weight, residual, gain, wide):
     tokens, n_feat = queries.shape
     share, d = residual.shape
     heads = n_feat // HEAD_SIZE
@@ -770,7 +853,7 @@
     rows = out_weight.shape[0]
     return pl.pallas_call(
         functools.partial(fused_kernel, features=d),
-        in_specs=[any_spec] * 5 + [vmem],
+        in_specs=[any_spec] * 5 + [vmem] * 2,
         out_specs=[any_spec, vmem, vmem, vmem],
         out_shape=[
             jax.ShapeDtypeStruct((share, d), f32),
@@ -792,6 +875,16 @@
             pltpu.VMEM((2, share, n_feat), bf16),
             pltpu.VMEM((share, LANES), f32),
             pltpu.VMEM((3, 8, 8, LANES), f32),
+            pltpu.VMEM((4, tokens, tokens), f32),
+            pltpu.VMEM((4, tokens, tokens), f32),
+            pltpu.VMEM((tokens, LANES), f32),
+            pltpu.VMEM((tokens, LANES), f32),
+            pltpu.VMEM((tokens, tokens), bf16),
+            pltpu.VMEM((tokens, LANES), f32),
+            pltpu.VMEM((tokens, HEAD_SIZE), f32),
+            pltpu.VMEM((4, share, 2 * LANES), f32),
+            pltpu.VMEM((4, share, 2 * LANES), f32),
+            pltpu.VMEM((d // LANES, LANES), f32),
             dma((3 + heads,)),
             dma((tiles,)),
             dma((tiles,)),
@@ -813,19 +906,14 @@
             collective_id=0, has_side_effects=True, vmem_limit_bytes=60 * 1024 * 1024
         ),
         name="fused",
-    )(queries, keys, values, out_weight, residual, gain)
-
-
-def two_parts(x):
-    high = x.astype(jnp.bfloat16)
-    low = (x - high.astype(jnp.float32)).astype(jnp.bfloat16)
-    return jnp.concatenate([high, low], axis=1)
+    )(queries, keys, values, out_weight, residual, gain, wide)
 
 
 def final_fast_kernel(top_ref, hid_ref, rstd_ref, bm_ref, gain_ref, wide_ref, new_ref, out_ref):
-    rows = hid_ref.shape[0]
+    rows, d = hid_ref.shape
     groups = bm_ref.shape[0]
     inv, tensor_scale = scales_of(top_ref[0:1, :])
+    gains = gain_ref[...].astype(jnp.float32)
     rstd = rstd_ref[...]
     rates, spacings = [], []
     for g in range(groups):
@@ -841,23 +929,22 @@
         rate = jnp.dot(rates, wide, preferred_element_type=jnp.float32)
         spacing = jnp.dot(spacings, wide, preferred_element_type=jnp.float32)
         for g in range(groups):
-            lo = (g * BLOCK // 2 + v) * width
+            pair = g * (BLOCK // 4) + v // 2 + v % 2 * (d // (2 * width))
+            lo = pair * width
             h = hid_ref[:, lo : lo + width]
             new_ref[:, lo : lo + width] = h.astype(jnp.bfloat16)
-            u = (h * gain_ref[:, lo : lo + width]) * rate[g * rows : (g + 1) * rows]
+            gain = jnp.concatenate([gains[2 * pair + t : 2 * pair + t + 1] for t in (0, 1)], axis=1)
+            u = (h * gain) * rate[g * rows : (g + 1) * rows]
             payload = soft_grid(u).astype(jnp.bfloat16).astype(jnp.float32)
             out_ref[:, lo : lo + width] = (payload * spacing[g * rows : (g + 1) * rows]).astype(
                 jnp.bfloat16
             )
 
 
-def final_fast(top, hidden, rstd, block_max, gain):
+def final_fast(top, hidden, rstd, block_max, gain, wide):
     tokens, d = hidden.shape
+    rows = 64
     groups = block_max.shape[0]
-    rows = 64
-    src = np.arange(2 * LANES)[:, None] % LANES
-    dst = np.arange(BLOCK * LANES)[None, :]
-    wide = jnp.asarray(src == dst % LANES // BLOCK * BLOCK + dst // LANES, jnp.bfloat16)
     line = pl.BlockSpec((rows, d), lambda i: (i, 0))
     return pl.pallas_call(
         final_fast_kernel,
@@ -867,7 +954,7 @@
             line,
             pl.BlockSpec((rows, LANES), lambda i: (i, 0)),
             pl.BlockSpec((groups, rows, LANES), lambda i: (0, i, 0)),
-            pl.BlockSpec((1, d), lambda i: (0, 0)),
+            pl.BlockSpec((d // LANES, LANES), lambda i: (0, 0)),
             pl.BlockSpec((2 * LANES, BLOCK * LANES), lambda i: (0, 0)),
         ],
         out_specs=[line, line],
@@ -883,6 +970,7 @@
         and sizes["seq"] == 4
         and sizes["dp"] % 2 == 0
         and keys.shape[1] == HEAD_SIZE
+        and queries.shape[1] == 4 * HEAD_SIZE
         and out_weight.shape[1] % (64 * LANES) == 0
         and out_weight.shape[0] == queries.shape[1]
         and out_weight.shape[0] % LANES == 0
@@ -894,9 +982,10 @@
 def local(queries, keys, values, out_weight, residual, norm_gain):
     if not fits_fused(queries, keys, out_weight, residual):
         return general(queries, keys, values, out_weight, residual, norm_gain)
-    gain = norm_gain.astype(jnp.float32).reshape(1, -1)
-    hidden, rstd, top, block_max = fused(queries, keys, values, out_weight, residual, gain)
-    return tuple(final_fast(top, hidden, rstd, block_max, gain))
+    gain = norm_gain.reshape(-1, LANES)
+    wide = spread_matrix()
+    hidden, rstd, top, block_max = fused(queries, keys, values, out_weight, residual, gain, wide)
+    return tuple(final_fast(top, hidden, rstd, block_max, gain, wide))
 
 
 def solution(mesh):

time: 78.3 us -> 71.7 us (0.916)
  Pallas kernels: 76 us -> 70.8 us
  other arithmetic: 1.33 us -> 0 us
    pallas_call x1, Pallas kernels: 64.8 us -> 59.7 us  [fused(): pl.pallas_call(functools.partial(fused_kernel, features=d), in_specs=[any...]
    reshape x1 -> x0, other arithmetic: 1.33 us -> none  [local(): gain = norm_gain.astype(jnp.float32).reshape(1, -1)]
where the time goes in v3:
time: 71.7 us; the launch traced here: 71.5 us
  Pallas kernels  70.8 us (99%)
    pallas_call x1, Pallas kernels, fused(): pl.pallas_call(functools.partial(fused_kernel, features=d), in_specs=[any...  59.7 us
    pallas_call x1, Pallas kernels, final_fast(): pl.pallas_call(final_fast_kernel, grid=(tokens // rows,), in_specs=[pl.Bl...  11.1 us

profile of v3, /device:TPU:0, one launch (start us, length us, event | category | flops | bytes accessed | tf_op | source)
XLA Modules:
  0.0 71.5 jit_solution(7278421975299566642)
XLA Ops:
  0.6 59.7 %fused.1 = (f32[256,8192]{1,0:T(8,128)}, f32[256,128]{1,0:T(8,128)}, f32[8,128]{1,0:T(8,128)}, f32[4,256,128]{2,1,0:T(8,128)}) custom-call(bf16[512,512]{1,0:T(8,128)(2,1)} %q_hbm.1, bf16[512,128]{1,0:T(8,128)(2,1)} %k_hbm.1, bf16[512,128]{1,0:T(8,128)(2,1)} %v_hbm.1, bf16[512,8192]{1,0:T(8,128)(2,1)} %w_hbm.1, bf16[256,8192]{1,0:T(8,128)(2,1)} %res_hbm.1, ...), custom_call_target="tpu_custom_call" | custom-call | tf_op jit(solution)/shard_map/fused/pallas_call | solution.py:854
  60.3 11.1 %final_fast.1 = (bf16[256,8192]{1,0:T(8,128)(2,1)}, bf16[256,8192]{1,0:T(8,128)(2,1)}) custom-call(f32[8,128]{1,0:T(8,128)} %get-tuple-element.6.top_ref, f32[256,8192]{1,0:T(8,128)} %get-tuple-element.7.hid_ref, f32[256,128]{1,0:T(8,128)} %get-tuple-element.8.rstd_ref, f32[4,256,128]{2,1,0:T(8,128)} %get-tuple-element.9.bm_ref, bf16[64,128]{1,0:T(8,128)(2,1)} %bitcast.2, ...), custom_call_target="tpu_custom_call" | custom-call | tf_op jit(solution)/shard_map/final_fast/pallas_call | solution.py:949

commit v4 on v3

--- a/solution.py
+++ b/solution.py
@@ -15,6 +15,7 @@
 neg_large = -1e30
 LANES = 128
 AHEAD = 2
+AHEAD_PAIRS = 2
 RAW = 2
 ROUND_BIG = 25165824.0
 Q_COEFFS = (0.8999997814, -0.5804296733, 0.1500389216, -0.0212977078, 0.0016888914)
@@ -283,16 +284,43 @@
     return (new_residual, next_input)
 
 
-def quant_tile(src, dst, inv, tensor_scale):
+def row_maxima(parts):
+    row = lax.broadcasted_iota(jnp.int32, parts[0].shape, 0)
+    half = len(parts) // 2
+    low = row < 4
+    parts = [
+        jnp.maximum(jnp.where(low, a, b), pltpu.roll(jnp.where(low, b, a), 4, 0))
+        for a, b in zip(parts[:half], parts[half:])
+    ]
+    for s in (2, 1):
+        half //= 2
+        even = row // s % 2 == 0
+        parts = [
+            jnp.maximum(
+                jnp.where(even, a, b),
+                jnp.where(even, pltpu.roll(a, 8 - s, 0), pltpu.roll(b, s, 0)),
+            )
+            for a, b in zip(parts[:half], parts[half:])
+        ]
+    return parts[0]
+
+
+def quant_tile(src, dst, inv, tensor_scale, rate_buf, space_buf):
     rows = src.shape[0]
-    step = 128 if rows % 128 == 0 else BLOCK
-    for lo in range(0, rows, step):
-        x = src[lo : lo + step, :].astype(jnp.float32).reshape(step // BLOCK, BLOCK, LANES)
-        block_max = jnp.max(jnp.abs(x), axis=1, keepdims=True)
-        scale = jnp.maximum(block_max * inv, scale_floor).astype(jnp.bfloat16)
+    for lo in range(0, rows, 8 * BLOCK):
+        parts = []
+        for b in range(lo, lo + 8 * BLOCK, BLOCK):
+            x = jnp.abs(src[b : b + BLOCK, :].astype(jnp.float32))
+            parts.append(jnp.maximum(x[:8], x[8:]))
+        scale = jnp.maximum(row_maxima(parts) * inv, scale_floor).astype(jnp.bfloat16)
         spacing = scale.astype(jnp.float32) * tensor_scale
-        payload = soft_grid(x * (1.0 / spacing)).astype(jnp.bfloat16).astype(jnp.float32)
-        dst[lo : lo + step, :] = (payload * spacing).reshape(step, LANES).astype(jnp.bfloat16)
+        rate_buf[lo // BLOCK : lo // BLOCK + 8, :] = 1.0 / spacing
+        space_buf[lo // BLOCK : lo // BLOCK + 8, :] = spacing
+    for b in range(0, rows, BLOCK):
+        n = b // BLOCK
+        x = src[b : b + BLOCK, :].astype(jnp.float32)
+        payload = soft_grid(x * rate_buf[n : n + 1, :]).astype(jnp.bfloat16).astype(jnp.float32)
+        dst[b : b + BLOCK, :] = (payload * space_buf[n : n + 1, :]).astype(jnp.bfloat16)
 
 
 def scales_of(top):
@@ -338,7 +366,7 @@
     q_hbm, k_hbm, v_hbm, w_hbm, res_hbm, gain_ref, wide_ref,
     hid_hbm, rstd_ref, top_ref, bm_ref,
     q_buf, kv_buf, raw_own, raw_peer, w_own, w_peer, res_buf, hid_buf,
-    act_full, act_peer, act_q, square_sum, peaks,
+    act_full, act_peer, act_q, square_sum, peaks, rate_buf, space_buf,
     score_a, score_b, top_a, top_b, weights, total, acc, parts_a, parts_b, gain_f,
     local_sem, load_sem, recv_sem, x_sem, y_sem, z_sem,
     kv_send, kv_recv, peak_send, peak_recv, act_sem,
@@ -456,19 +484,25 @@
     other = y * 2 + 1 - core
     far = (1 - y) * 2 + core
     far_other = (1 - y) * 2 + 1 - core
-    kv_y = remote(kv_buf.at[seq], kv_buf.at[seq], kv_send.at[0], kv_recv.at[seq], y_dev)
-    kv_s = remote(kv_buf.at[seq], kv_buf.at[seq], kv_send.at[1], kv_recv.at[seq], s_dev)
-    kv_f = remote(kv_buf.at[far], kv_buf.at[far], kv_send.at[2], kv_recv.at[far], s_dev)
-    kv_y.start()
-    kv_s.start()
-
-    def wait_load(n, c):
-        load(load_order(n)).wait()
-        return c
-
-    wait_load(0, 0)
+    def kv_copy(part, n, slot, dev):
+        ref = kv_buf.at[slot, part]
+        return remote(ref, ref, kv_send.at[part, n], kv_recv.at[part, slot], dev)
+
+    kv_sends = [kv_copy(part, n, seq, dev) for part in range(2) for n, dev in ((0, y_dev), (1, s_dev))]
+    for c in kv_sends:
+        c.start()
+    kv_onward = [kv_copy(part, 2, far, s_dev) for part in range(2)]
+
+    def kv_pass(part):
+        kv_copy(part, 0, far, y_dev).wait_recv()
+        kv_onward[part].start()
+
+    def kv_rest(part):
+        for slot in (other, far_other):
+            kv_copy(part, 1, slot, s_dev).wait_recv()
+
+    load(load_order(0)).wait()
     x_send(0).start()
-    lax.fori_loop(1, tiles, wait_load, 0)
 
     def peak_exchange(kind, value, members):
         me = seq * 2 + tp
@@ -501,7 +535,16 @@
     def tile_top(j, m):
         high, low = m
         for t in range(4):
-            x = raw_own[4 * j + t].reshape(-1, 8 * BLOCK, LANES)
+            n = load_order(4 * j + t)
+            if t:
+                load(n).wait()
+            else:
+                @pl.when(j > 0)
+                def _():
+                    load(n).wait()
+
+        for t in range(4):
+            x = raw_own[load_order(4 * j + t)].reshape(-1, 8 * BLOCK, LANES)
             high = jnp.maximum(high, jnp.max(x, axis=0))
             low = jnp.minimum(low, jnp.min(x, axis=0))
         return high, low
@@ -526,7 +569,7 @@
 
     def own_pair(p):
         for t in range(2):
-            quant_tile(raw_own.at[2 * p + t], w_own.at[col0 + 2 * p + t], w_inv, w_scale)
+            quant_tile(raw_own.at[2 * p + t], w_own.at[col0 + 2 * p + t], w_inv, w_scale, rate_buf.at[t], space_buf.at[t])
         own_copy(p).start()
 
     def own_range(first, count):
@@ -537,16 +580,16 @@
         lax.fori_loop(0, count, body, 0)
 
     half = group_pairs
+    kv_pass(0)
     own_range(g_mine * half + 1, 1)
     forward(0)
     own_range(g_mine * half + 2, half - 2)
-    remote(kv_buf.at[far], kv_buf.at[far], kv_send.at[0], kv_recv.at[far], y_dev).wait_recv()
-    kv_f.start()
+    forward(1)
+    kv_pass(1)
 
     for c in q_loads:
         c.wait()
-    for slot in (other, far_other):
-        remote(kv_buf.at[slot], kv_buf.at[slot], kv_send.at[0], kv_recv.at[slot], s_dev).wait_recv()
+    kv_rest(0)
 
     rate = HEAD_SIZE ** (-0.5) * 1.4426950408889634
 
@@ -612,14 +655,14 @@
     )
     jobs = [(theirs, 0), (theirs, 2), (mine, 0), (mine, 2)]
     jobs = [j + ((score_a, top_a) if n % 2 == 0 else (score_b, top_b)) for n, j in enumerate(jobs)]
-    forward(1)
     attend(None, jobs[0])
+    kv_rest(1)
+    a_top = attend(jobs[0], jobs[1])
     forward(2)
-    a_top = attend(jobs[0], jobs[1])
+    a_top = jnp.maximum(a_top, attend(jobs[1], jobs[2]))
+    act_copy.start()
     relay(0)
     relay(1)
-    a_top = jnp.maximum(a_top, attend(jobs[1], jobs[2]))
-    act_copy.start()
     a_top = jnp.maximum(a_top, attend(jobs[2], jobs[3]))
     a_top = jnp.maximum(a_top, attend(jobs[3], None))
     a_top = jnp.full((8, LANES), jnp.max(a_top), jnp.float32)
@@ -632,7 +675,6 @@
     relay(2)
     own_range(g_z * half, half)
     relay(3)
-    forward(5)
     own_range(g_d * half, half - 1)
     square_sum[...] = jnp.zeros_like(square_sum)
 
@@ -657,12 +699,12 @@
         elif p:
             wait_tile(2 * lp + p - 1)
         for t in range(2):
-            quant_tile(raw_peer.at[2 * lp + t], w_peer.at[col0 + 2 * lp + t], w_inv, w_scale)
+            quant_tile(raw_peer.at[2 * lp + t], w_peer.at[col0 + 2 * lp + t], w_inv, w_scale, rate_buf.at[t], space_buf.at[t])
         peer_copy(lp).start()
 
     for p in (0, 1):
         take_raw(p)
-    forward(6)
+    forward(5)
     relay(4)
     for p in (2, 3 * group_pairs):
         take_raw(p)
@@ -768,15 +810,14 @@
 
         peer_copy(lp).start()
 
+    forward(6)
     res_load.wait()
     gain_f[...] = gain_ref[...].astype(jnp.float32)
-    forward(7)
-    relay(5)
 
     def step(p, parts, before):
-        @pl.when((p > 1) * (p < pairs - 1) * (p + 1 != 3 * group_pairs))
+        @pl.when((p > 2 - AHEAD_PAIRS) * (p < pairs - AHEAD_PAIRS) * (p + AHEAD_PAIRS != 3 * group_pairs))
         def _():
-            take(p + 1)
+            take(p + AHEAD_PAIRS)
 
         lp = local_pair(p)[0]
         sl = pl.ds(other0 + 2 * lp, 2)
@@ -791,6 +832,14 @@
     def two_steps(r, c):
         p = 2 * r + 1
 
+        @pl.when(r == 0)
+        def _():
+            relay(5)
+
+        @pl.when(r == 1)
+        def _():
+            forward(7)
+
         step(p, parts_b, parts_a)
 
         step(p + 1, parts_a, parts_b)
@@ -806,9 +855,8 @@
     n_top = jnp.max(jnp.max(bm_ref[...], axis=0) * rstd)
     finish_n, n_sends = peak_exchange(2, jnp.full((8, LANES), n_top, jnp.float32), team)
 
-    kv_y.wait_send()
-    kv_s.wait_send()
-    kv_f.wait_send()
+    for c in kv_sends + kv_onward:
+        c.wait_send()
     act_copy.wait_send()
     for c in w_sends + a_sends:
         c.wait_send()
@@ -875,6 +923,8 @@
             pltpu.VMEM((2, share, n_feat), bf16),
             pltpu.VMEM((share, LANES), f32),
             pltpu.VMEM((3, 8, 8, LANES), f32),
+            pltpu.VMEM((2, rows // BLOCK, LANES), f32),
+            pltpu.VMEM((2, rows // BLOCK, LANES), f32),
             pltpu.VMEM((4, tokens, tokens), f32),
             pltpu.VMEM((4, tokens, tokens), f32),
             pltpu.VMEM((tokens, LANES), f32),
@@ -891,8 +941,8 @@
             dma((group + group // 4,)),
             dma((group + 3 * group // 8,)),
             dma((group + 3 * group // 8,)),
-            dma((3,)),
-            dma((4,)),
+            dma((2, 3)),
+            dma((2, 4)),
             dma((3, 7)),
             dma((3, 8)),
             dma((2,)),

time: 71.7 us -> 69.9 us (0.975)
  Pallas kernels: 70.8 us -> 69 us
    pallas_call x1, Pallas kernels: 59.7 us -> 57.9 us  [fused(): pl.pallas_call(functools.partial(fused_kernel, features=d), in_specs=[any...]
where the time goes in v4:
time: 69.9 us; the launch traced here: 69.6 us
  Pallas kernels  69 us (99%)
    pallas_call x1, Pallas kernels, fused(): pl.pallas_call(functools.partial(fused_kernel, features=d), in_specs=[any...  57.9 us
    pallas_call x1, Pallas kernels, final_fast(): pl.pallas_call(final_fast_kernel, grid=(tokens // rows,), in_specs=[pl.Bl...  11.1 us

profile of v4, /device:TPU:0, one launch (start us, length us, event | category | flops | bytes accessed | tf_op | source)
XLA Modules:
  0.0 69.6 jit_solution(14739684383088495480)
XLA Ops:
  0.6 57.9 %fused.1 = (f32[256,8192]{1,0:T(8,128)}, f32[256,128]{1,0:T(8,128)}, f32[8,128]{1,0:T(8,128)}, f32[4,256,128]{2,1,0:T(8,128)}) custom-call(bf16[512,512]{1,0:T(8,128)(2,1)} %q_hbm.1, bf16[512,128]{1,0:T(8,128)(2,1)} %k_hbm.1, bf16[512,128]{1,0:T(8,128)(2,1)} %v_hbm.1, bf16[512,8192]{1,0:T(8,128)(2,1)} %w_hbm.1, bf16[256,8192]{1,0:T(8,128)(2,1)} %res_hbm.1, ...), custom_call_target="tpu_custom_call" | custom-call | tf_op jit(solution)/shard_map/fused/pallas_call | solution.py:902
  58.5 11.1 %final_fast.1 = (bf16[256,8192]{1,0:T(8,128)(2,1)}, bf16[256,8192]{1,0:T(8,128)(2,1)}) custom-call(f32[8,128]{1,0:T(8,128)} %get-tuple-element.6.top_ref, f32[256,8192]{1,0:T(8,128)} %get-tuple-element.7.hid_ref, f32[256,128]{1,0:T(8,128)} %get-tuple-element.8.rstd_ref, f32[4,256,128]{2,1,0:T(8,128)} %get-tuple-element.9.bm_ref, bf16[64,128]{1,0:T(8,128)(2,1)} %bitcast.2, ...), custom_call_target="tpu_custom_call" | custom-call | tf_op jit(solution)/shard_map/final_fast/pallas_call | solution.py:999
